TPU v7x, 128 devices: a whole 4x4x4 slice. The times are simulated.
128 devices in a mesh: trade: 4 (over z), node: 32 (over x, y, core).
Axes of the slice: x: 4, y: 4, z: 4, core: 2. Of those that a mesh axis runs over, the one named last changes fastest.
Arguments:
- values_in: float32 [1024, 65536], P('trade', 'node'), may hold values from 0 to 1
- prob_up: float32 [16, 65536], P(None, 'node'), may hold values from 0.1 to 0.3
- prob_down: float32 [16, 65536], P(None, 'node'), may hold values from 0.1 to 0.3
- discount: float32 [16, 65536], P(None, 'node'), may hold values from 0.9 to 1
- swap_rate: float32 [16, 65536], P(None, 'node'), may hold values from -3 to 3
- annuity: float32 [16, 65536], P(None, 'node'), may hold values from 0.5 to 2
- state_price: float32 [65536], P('node'), may hold values from 7.6293945e-06 to 3.0517578e-05
- exercise_step: int32 [1024, 4], P('trade'), may hold values from 0 to 15
- strike_bucket: int32 [1024], P('trade'), may hold values from 0 to 63
- notional_sign: int32 [1024], P('trade'), may hold values from 0 to 1
- strike_table: float32 [64], replicated, may hold values from -0.5 to 0.5
Outputs:
- values_out: float32 [1024, 65536], P(('trade', 'node'))
- prices: float32 [1024], P(('trade', 'node'))
- portfolio: float32 [], replicated
All inputs are finite; a program needn't handle non-finite values.
Results may differ from a plain program's by a relative error of at most 0.0003.
Values sent between devices are 32-bit elements; how exact they have to be, the bound alone decides.
No kernel may reach another device: no remote copies, remote signals or barrier semaphores. Data moves between devices by JAX's collectives and lax.ppermute only.
A program may use at most 128 MiB of HBM per device.

v0:
```python
import jax
import jax.numpy as jnp
from jax import lax
from jax.sharding import Mesh
from jax.sharding import PartitionSpec as P

NODE = ("node_0", "node_1", "node_2")
TRADE_NODE = ("trade", "node_0", "node_1", "node_2")


def extended(x, sides, width):
    for axis, dim in sides:
        devices, length = (lax.axis_size(axis), x.shape[dim])
        up = [(i, (i + 1) % devices) for i in range(devices - 1)]
        down = [(j, i) for i, j in up]
        last = lax.slice_in_dim(x, length - width, length, axis=dim)
        leading = lax.slice_in_dim(x, 0, width, axis=dim)
        before = lax.ppermute(last, axis, up)
        after = lax.ppermute(leading, axis, down)
        x = jnp.concatenate([before, x, after], axis=dim)
    return x


def cut_along(x, dim, devices):
    dims = x.shape
    tiles = x.reshape(*dims[:dim], devices, dims[dim] // devices, *dims[dim + 1 :])
    return jnp.moveaxis(tiles, dim, 0)


def summed_on_arrival(x, axis, dim):
    devices = lax.axis_size(axis)
    tiles = lax.all_to_all(cut_along(x, dim, devices), axis, 0, 0, tiled=True)
    return jnp.sum(tiles, axis=0)


def one_axis_at_a_time(x, axes):
    for axis in axes:
        x = lax.psum(x, axis)
    return x


def strikes_of(bucket, strike_table):
    levels = lax.broadcasted_iota(jnp.int32, (1, strike_table.shape[0]), 1)
    return jnp.sum(
        jnp.where(
            bucket[:, None] == levels, strike_table[None, :], jnp.zeros((), strike_table.dtype)
        ),
        axis=1,
    )


def roll_once(padded, prob_up, prob_down, discount_row):
    middle = 1.0 - prob_up - prob_down
    return discount_row * (
        prob_up * padded[:, 2:] + middle * padded[:, 1:-1] + prob_down * padded[:, :-2]
    )


def exercise(values, active, strike, signs, swap_row, annuity_row):
    payoff = signs[:, None] * annuity_row[None, :] * (swap_row[None, :] - strike[:, None])
    return jnp.where(active[:, None], jnp.maximum(values, payoff), values)


def roll_front(
    values,
    prob_up,
    prob_down,
    discount,
    swap_rate,
    annuity,
    exercise_step,
    strike,
    signs,
    split_step,
):
    node_dev = values.shape[1]
    node_count = lax.axis_size(NODE)
    rim_depth = 4
    stacked = jnp.stack([prob_up, prob_down, discount, swap_rate, annuity])
    lattice_rim = extended(stacked, ((NODE, 2),), rim_depth)
    offset = lax.axis_index(NODE) * node_dev - rim_depth
    position = offset + lax.broadcasted_iota(jnp.int32, (node_dev + 2 * rim_depth,), 0)
    inside = (position >= 0) & (position < node_dev * node_count)
    for block_index in range(split_step // rim_depth):
        padded = extended(values, ((NODE, 1),), rim_depth)
        for inner in range(rim_depth):
            step = block_index * rim_depth + inner
            first_cell = inner + 1
            cell_count = node_dev + 2 * (rim_depth - inner) - 2
            coefs = lattice_rim[:, step, first_cell : first_cell + cell_count]
            rolled = roll_once(padded, coefs[0], coefs[1], coefs[2])
            active = jnp.any(exercise_step == step, axis=1)
            rolled = exercise(rolled, active, strike, signs, coefs[3], coefs[4])
            padded = jnp.where(inside[first_cell : first_cell + cell_count][None, :], rolled, 0.0)
        values = padded
    return values


def to_trade_rows(values):
    node_count = lax.axis_size(NODE)
    node_dev = values.shape[1]
    row_count = values.shape[0] // node_count
    blocks = values.reshape(node_count, row_count, node_dev)
    moved = lax.all_to_all(blocks, NODE, split_axis=0, concat_axis=2, tiled=True)
    return moved.reshape(row_count, node_dev * node_count)


def local(
    values_in,
    prob_up,
    prob_down,
    discount,
    swap_rate,
    annuity,
    state_price,
    exercise_step,
    strike_bucket,
    notional_sign,
    strike_table,
):
    step_count = prob_up.shape[0]
    strike = strikes_of(strike_bucket, strike_table)
    signs = (2 * notional_sign - 1).astype(jnp.float32)
    values = roll_front(
        values_in,
        prob_up,
        prob_down,
        discount,
        swap_rate,
        annuity,
        exercise_step,
        strike,
        signs,
        step_count,
    )
    partial_prices = jnp.sum(values * state_price[None, :], axis=1)
    values = to_trade_rows(values)
    prices = summed_on_arrival(partial_prices, NODE, 0)
    portfolio = one_axis_at_a_time(jnp.sum(prices), TRADE_NODE) / values_in.shape[0]
    return (values, prices, portfolio)


def solution(mesh):
    split = Mesh(
        mesh.devices.reshape(mesh.shape["trade"], 4, 4, 2), ("trade", "node_0", "node_1", "node_2")
    )
    in_specs = (
        P("trade", NODE),
        P(None, NODE),
        P(None, NODE),
        P(None, NODE),
        P(None, NODE),
        P(None, NODE),
        P(NODE),
        P("trade", None),
        P("trade"),
        P("trade"),
        P(),
    )
    out_specs = (P(TRADE_NODE, None), P(TRADE_NODE), P())
    return jax.shard_map(local, mesh=split, in_specs=in_specs, out_specs=out_specs, check_vma=False)
```

profile of v0, /device:TPU:1, one launch (start us, length us, event | category | flops | bytes accessed | tf_op | source)
XLA Modules:
  0.0 179.0 jit_solution(3867763831313351278)
XLA Ops:
  0.7 1.1 fusion.72
  1.7 3.3 %collective-permute-start.3 = (f32[256,4]{1,0:T(8,128)S(1)}, f32[256,4]{1,0:T(8,128)S(1)}, u32[]{:S(2)}, u32[]{:S(2)}) collective-permute-start(f32[256,4]{1,0:T(8,128)S(1)} %get-tuple-element.86), channel_id=1, source_target_pairs={{1,0},{2,1},{3,2},{4,3},{5,4},{6,5},{7,6},{8,7},{9,8},{10,9},{11,1... | collective-permute-start | bytes 12296 | tf_op jit(solution)/shard_map/ppermute | solution.py:19
  5.0 3.2 %collective-permute-start.2 = (f32[256,4]{1,0:T(8,128)S(1)}, f32[256,4]{1,0:T(8,128)S(1)}, u32[]{:S(2)}, u32[]{:S(2)}) collective-permute-start(f32[256,4]{1,0:T(8,128)S(1)} %get-tuple-element.87), channel_id=1, source_target_pairs={{0,1},{1,2},{2,3},{3,4},{4,5},{5,6},{6,7},{7,8},{8,9},{9,10},{10,1... | collective-permute-start | bytes 12296 | tf_op jit(solution)/shard_map/ppermute | solution.py:18
  8.2 0.9 constant_dynamic-update-slice_fusion.4
  9.2 0.9 constant_dynamic-update-slice_fusion.3
  10.1 0.9 constant_dynamic-update-slice_fusion.2
  11.0 0.9 constant_dynamic-update-slice_fusion.1
  11.9 0.9 constant_dynamic-update-slice_fusion
  12.9 1.9 %collective-permute-start.1 = (f32[5,16,4]{2,1,0:T(8,128)S(1)}, f32[5,16,4]{2,1,0:T(8,128)S(1)}, u32[]{:S(2)}, u32[]{:S(2)}) collective-permute-start(f32[5,16,4]{2,1,0:T(8,128)S(1)} %get-tuple-element.88), channel_id=1, source_target_pairs={{1,0},{2,1},{3,2},{4,3},{5,4},{6,5},{7,6},{8,7},{9,8},{10,9},{11,1... | collective-permute-start | bytes 3848 | tf_op jit(solution)/shard_map/ppermute | solution.py:19
  14.8 3.6 %collective-permute-start = (f32[5,16,4]{2,1,0:T(8,128)S(1)}, f32[5,16,4]{2,1,0:T(8,128)S(1)}, u32[]{:S(2)}, u32[]{:S(2)}) collective-permute-start(f32[5,16,4]{2,1,0:T(8,128)S(1)} %get-tuple-element.89), channel_id=1, source_target_pairs={{0,1},{1,2},{2,3},{3,4},{4,5},{5,6},{6,7},{7,8},{8,9},{9,10},{10,1... | collective-permute-start | bytes 3848 | tf_op jit(solution)/shard_map/ppermute | solution.py:18
  18.5 0.7 add_convert_fusion
  19.2 1.4 compare_reduce_fusion.15
  20.6 1.6 fusion.77
  22.1 1.6 fusion.78
  23.7 1.6 fusion.74
  25.2 1.0 fusion.76
  26.2 1.0 fusion.75
  29.7 0.7 slice.776
  31.2 1.1 slice_reduce_fusion.55
  32.3 1.1 slice_reduce_fusion.57
  33.4 1.1 slice_reduce_fusion.59
  35.2 0.6 subtract_subtract_fusion.5
  35.8 0.6 subtract_subtract_fusion.8
  36.4 0.6 subtract_subtract_fusion.11
  37.6 0.6 subtract_subtract_fusion
  38.2 0.6 subtract_subtract_fusion.6
  39.4 3.0 %concatenate.16 = f32[256,2056]{1,0:T(8,128)S(1)} concatenate(f32[256,4]{1,0:T(8,128)S(1)} %collective-permute-done.2, f32[256,2048]{1,0:T(8,128)} %param.11, f32[256,4]{1,0:T(8,128)S(1)} %collective-permute-done.3), dimensions={1} | concatenate | bytes 4210688 | tf_op jit(solution)/shard_map/concatenate | solution.py:20
  42.4 2.2 %fusion = f32[256,2054]{1,0:T(8,128)S(1)} fusion(f32[256,2056]{1,0:T(8,128)S(1)} %concatenate.16, f32[256]{0:T(256)S(1)} %select_reduce_fusion, f32[2054]{0:T(1024)} %get-tuple-element.51, f32[2054]{0:T(1024)} %get-tuple-element.52, f32[256]{0:T(256)S(1)} %add_convert_fusion, f32[2054]{0:T(1024)S(1)} %get-tuple-element.53, ...), kind=kLoop, calls=%fused_computation.16 | loop fusion | flops 6309888 | bytes 8466838 | tf_op jit(solution)/shard_map/jit(_where)/select_n | solution.py:94
  44.7 1.4 fusion.1
  46.3 1.4 fusion.2
  47.8 1.4 fusion.48
  49.3 1.9 %collective-permute-start.5 = (f32[256,4]{1,0:T(8,128)S(1)}, f32[256,4]{1,0:T(8,128)S(1)}, u32[]{:S(2)}, u32[]{:S(2)}) collective-permute-start(f32[256,4]{1,0:T(8,128)S(1)} %get-tuple-element.84), channel_id=1, source_target_pairs={{1,0},{2,1},{3,2},{4,3},{5,4},{6,5},{7,6},{8,7},{9,8},{10,9},{11,1... | collective-permute-start | bytes 12296 | tf_op jit(solution)/shard_map/ppermute | solution.py:19
  51.2 3.8 %collective-permute-start.4 = (f32[256,4]{1,0:T(8,128)S(1)}, f32[256,4]{1,0:T(8,128)S(1)}, u32[]{:S(2)}, u32[]{:S(2)}) collective-permute-start(f32[256,4]{1,0:T(8,128)S(1)} %get-tuple-element.85), channel_id=1, source_target_pairs={{0,1},{1,2},{2,3},{3,4},{4,5},{5,6},{6,7},{7,8},{8,9},{9,10},{10,1... | collective-permute-start | bytes 12296 | tf_op jit(solution)/shard_map/ppermute | solution.py:18
  55.0 0.6 subtract_subtract_fusion.7
  55.7 1.1 collective-permute-done.4
  56.8 3.0 %concatenate.17 = f32[256,2056]{1,0:T(8,128)S(1)} concatenate(f32[256,4]{1,0:T(8,128)S(1)} %collective-permute-done.4, f32[256,2048]{1,0:T(8,128)} %copy-done.1, f32[256,4]{1,0:T(8,128)S(1)} %collective-permute-done.5), dimensions={1} | concatenate | bytes 4210688 | tf_op jit(solution)/shard_map/concatenate | solution.py:20
  59.9 1.4 fusion.3
  61.4 1.4 fusion.4
  63.0 1.4 fusion.5
  64.5 1.4 fusion.49
  66.0 1.9 %collective-permute-start.7 = (f32[256,4]{1,0:T(8,128)S(1)}, f32[256,4]{1,0:T(8,128)S(1)}, u32[]{:S(2)}, u32[]{:S(2)}) collective-permute-start(f32[256,4]{1,0:T(8,128)S(1)} %get-tuple-element.82), channel_id=1, source_target_pairs={{1,0},{2,1},{3,2},{4,3},{5,4},{6,5},{7,6},{8,7},{9,8},{10,9},{11,1... | collective-permute-start | bytes 12296 | tf_op jit(solution)/shard_map/ppermute | solution.py:19
  67.9 4.6 %collective-permute-start.6 = (f32[256,4]{1,0:T(8,128)S(1)}, f32[256,4]{1,0:T(8,128)S(1)}, u32[]{:S(2)}, u32[]{:S(2)}) collective-permute-start(f32[256,4]{1,0:T(8,128)S(1)} %get-tuple-element.83), channel_id=1, source_target_pairs={{0,1},{1,2},{2,3},{3,4},{4,5},{5,6},{6,7},{7,8},{8,9},{9,10},{10,1... | collective-permute-start | bytes 12296 | tf_op jit(solution)/shard_map/ppermute | solution.py:18
  73.0 1.2 collective-permute-done.6
  74.2 3.0 %concatenate.18 = f32[256,2056]{1,0:T(8,128)S(1)} concatenate(f32[256,4]{1,0:T(8,128)S(1)} %collective-permute-done.6, f32[256,2048]{1,0:T(8,128)} %copy-done, f32[256,4]{1,0:T(8,128)S(1)} %collective-permute-done.7), dimensions={1} | concatenate | bytes 4210688 | tf_op jit(solution)/shard_map/concatenate | solution.py:20
  77.3 1.4 fusion.6
  78.8 1.4 fusion.7
  80.4 1.5 fusion.8
  81.9 1.4 fusion.50
  83.4 1.9 %collective-permute-start.9 = (f32[256,4]{1,0:T(8,128)S(1)}, f32[256,4]{1,0:T(8,128)S(1)}, u32[]{:S(2)}, u32[]{:S(2)}) collective-permute-start(f32[256,4]{1,0:T(8,128)S(1)} %get-tuple-element.80), channel_id=1, source_target_pairs={{1,0},{2,1},{3,2},{4,3},{5,4},{6,5},{7,6},{8,7},{9,8},{10,9},{11,1... | collective-permute-start | bytes 12296 | tf_op jit(solution)/shard_map/ppermute | solution.py:19
  85.3 4.6 %collective-permute-start.8 = (f32[256,4]{1,0:T(8,128)S(1)}, f32[256,4]{1,0:T(8,128)S(1)}, u32[]{:S(2)}, u32[]{:S(2)}) collective-permute-start(f32[256,4]{1,0:T(8,128)S(1)} %get-tuple-element.81), channel_id=1, source_target_pairs={{0,1},{1,2},{2,3},{3,4},{4,5},{5,6},{6,7},{7,8},{8,9},{9,10},{10,1... | collective-permute-start | bytes 12296 | tf_op jit(solution)/shard_map/ppermute | solution.py:18
  90.4 1.2 collective-permute-done.8
  91.6 3.0 %concatenate.19 = f32[256,2056]{1,0:T(8,128)S(1)} concatenate(f32[256,4]{1,0:T(8,128)S(1)} %collective-permute-done.8, f32[256,2048]{1,0:T(8,128)} %copy-done.2, f32[256,4]{1,0:T(8,128)S(1)} %collective-permute-done.9), dimensions={1} | concatenate | bytes 4210688 | tf_op jit(solution)/shard_map/concatenate | solution.py:20
  94.6 1.5 fusion.9
  96.2 1.4 fusion.10
  97.8 1.4 fusion.11
  99.3 2.8 %multiply_reduce_fusion = (f32[256]{0:T(256)S(1)}, f32[256,2048]{1,0:T(8,128)}) fusion(f32[2048]{0:T(1024)S(1)} %copy-done.63, f32[256]{0:T(256)S(1)} %select_reduce_fusion, f32[2048]{0:T(1024)S(1)} %bitcast.61, f32[2048]{0:T(1024)S(1)} %bitcast.60, f32[256]{0:T(256)S(1)} %add_convert_fusion, f32[256,2050]{1,0:T(8,128)S(1)} %fusion.11, ...), kind=kLoop, calls=%fused_computation.128 | loop fusion | flops 7339776 | bytes 8451328 | tf_op jit(solution)/shard_map/reduce_sum | solution.py:136
  102.2 25.5 %all_to_all.24 = f32[32,1,8]{2,1,0:T(1,128)S(1)} all-to-all(f32[32,1,8]{2,1,0:T(1,128)S(1)} %bitcast.59), channel_id=1, replica_groups=mesh['trade'=4,'node_0'=4,'node_1'=4,'node_2'=2] {'node_0','node_1','nod..., dimensions={0} | all-to-all | bytes 2048 | tf_op jit(solution)/shard_map/all_to_all | solution.py:32
  127.6 4.3 %all-to-all-start = ((f32[32,8,2048]{2,1,0:T(8,128)}), f32[32,8,2048]{2,1,0:T(8,128)S(1)}, u32[]{:S(2)}, u32[]{:S(2)}) async-start(f32[32,8,2048]{2,1,0:T(8,128)} %bitcast.25), calls=%async_computation | async-start | bytes 4194304 | tf_op jit(solution)/shard_map/all_to_all | solution.py:104
  132.0 0.6 fusion.67
  132.6 10.9 %psum.28 = f32[]{:T(128)} all-reduce(f32[]{:T(128)} %get-tuple-element.60), channel_id=1, replica_groups=mesh['trade'=4,'node_0'=4,'node_1'=4,'node_2'=2] {'trade'}, use_global_device_ids=true, to_apply=%region_20.21 | all-reduce | flops 1 | bytes 8 | tf_op jit(solution)/shard_map/psum | solution.py:38
  143.5 16.7 %psum.29 = f32[]{:T(128)} all-reduce(f32[]{:T(128)} %psum.28), channel_id=1, replica_groups=mesh['trade'=4,'node_0'=4,'node_1'=4,'node_2'=2] {'node_0'}, use_global_device_ids=true, to_apply=%region_21.22 | all-reduce | flops 1 | bytes 8 | tf_op jit(solution)/shard_map/psum | solution.py:38
  160.2 9.0 %psum.30 = f32[]{:T(128)} all-reduce(f32[]{:T(128)} %psum.29), channel_id=1, replica_groups=mesh['trade'=4,'node_0'=4,'node_1'=4,'node_2'=2] {'node_1'}, use_global_device_ids=true, to_apply=%region_22.23 | all-reduce | flops 1 | bytes 8 | tf_op jit(solution)/shard_map/psum | solution.py:38
  169.3 6.6 %psum.31 = f32[]{:T(128)} all-reduce(f32[]{:T(128)} %psum.30), channel_id=1, replica_groups=mesh['trade'=4,'node_0'=4,'node_1'=4,'node_2'=2] {'node_2'}, use_global_device_ids=true, to_apply=%region_23.24 | all-reduce | flops 1 | bytes 8 | tf_op jit(solution)/shard_map/psum | solution.py:38
  176.5 1.3 copy.21
  (192 shorter events, 6.7 us)
Async XLA Ops:
  0.6 26.6 %copy-start.80 = (f32[64]{0:T(128)S(1)}, f32[64]{0:T(128)}, u32[]{:S(2)}) copy-start(f32[64]{0:T(128)} %param.21) | copy-start | bytes 772
  0.6 26.6 %copy-start.79 = (s32[256]{0:T(256)S(1)}, s32[256]{0:T(256)}, u32[]{:S(2)}) copy-start(s32[256]{0:T(256)} %param.19) | copy-start | bytes 3076
  1.7 37.7 %collective-permute-start.3 = (f32[256,4]{1,0:T(8,128)S(1)}, f32[256,4]{1,0:T(8,128)S(1)}, u32[]{:S(2)}, u32[]{:S(2)}) collective-permute-start(f32[256,4]{1,0:T(8,128)S(1)} %get-tuple-element.86), channel_id=1, source_target_pairs={{1,0},{2,1},{3,2},{4,3},{5,4},{6,5},{7,6},{8,7},{9,8},{10,9},{11,1... | collective-permute-start | bytes 12296 | tf_op jit(solution)/shard_map/ppermute | solution.py:19
  5.0 34.4 %collective-permute-start.2 = (f32[256,4]{1,0:T(8,128)S(1)}, f32[256,4]{1,0:T(8,128)S(1)}, u32[]{:S(2)}, u32[]{:S(2)}) collective-permute-start(f32[256,4]{1,0:T(8,128)S(1)} %get-tuple-element.87), channel_id=1, source_target_pairs={{0,1},{1,2},{2,3},{3,4},{4,5},{5,6},{6,7},{7,8},{8,9},{9,10},{10,1... | collective-permute-start | bytes 12296 | tf_op jit(solution)/shard_map/ppermute | solution.py:18
  12.9 17.7 %collective-permute-start.1 = (f32[5,16,4]{2,1,0:T(8,128)S(1)}, f32[5,16,4]{2,1,0:T(8,128)S(1)}, u32[]{:S(2)}, u32[]{:S(2)}) collective-permute-start(f32[5,16,4]{2,1,0:T(8,128)S(1)} %get-tuple-element.88), channel_id=1, source_target_pairs={{1,0},{2,1},{3,2},{4,3},{5,4},{6,5},{7,6},{8,7},{9,8},{10,9},{11,1... | collective-permute-start | bytes 3848 | tf_op jit(solution)/shard_map/ppermute | solution.py:19
  14.8 15.8 %collective-permute-start = (f32[5,16,4]{2,1,0:T(8,128)S(1)}, f32[5,16,4]{2,1,0:T(8,128)S(1)}, u32[]{:S(2)}, u32[]{:S(2)}) collective-permute-start(f32[5,16,4]{2,1,0:T(8,128)S(1)} %get-tuple-element.89), channel_id=1, source_target_pairs={{0,1},{1,2},{2,3},{3,4},{4,5},{5,6},{6,7},{7,8},{8,9},{9,10},{10,1... | collective-permute-start | bytes 3848 | tf_op jit(solution)/shard_map/ppermute | solution.py:18
  42.4 2.2 %copy-start.31 = (f32[2052]{0:T(1024)S(1)}, f32[2052]{0:T(1024)}, u32[]{:S(2)}) copy-start(f32[2052]{0:T(1024)} %get-tuple-element.32) | copy-start | bytes 24628
  42.4 2.2 %copy-start.32 = (f32[2052]{0:T(1024)S(1)}, f32[2052]{0:T(1024)}, u32[]{:S(2)}) copy-start(f32[2052]{0:T(1024)} %get-tuple-element.33) | copy-start | bytes 24628
  42.4 2.2 %copy-start.33 = (f32[2052]{0:T(1024)S(1)}, f32[2052]{0:T(1024)}, u32[]{:S(2)}) copy-start(f32[2052]{0:T(1024)} %get-tuple-element.36) | copy-start | bytes 24628
  42.4 2.2 %copy-start.46 = (f32[2052]{0:T(1024)S(1)}, f32[2052]{0:T(1024)}, u32[]{:S(2)}) copy-start(f32[2052]{0:T(1024)} %subtract_subtract_fusion.10) | copy-start | bytes 24628
  42.4 2.2 %copy-start.78 = (pred[256]{0:T(512)(128)(4,1)S(1)}, pred[256]{0:T(512)(128)(4,1)}, u32[]{:S(2)}) copy-start(pred[256]{0:T(512)(128)(4,1)} %get-tuple-element.77) | copy-start | bytes 772
  44.7 1.5 copy-start.34
  44.7 1.5 copy-start.35
  44.7 1.5 copy-start.36
  44.7 1.5 copy-start.40
  44.7 1.5 copy-start.77
  46.2 1.5 copy-start.3
  46.2 1.5 copy-start.53
  46.2 1.5 copy-start.60
  46.2 1.5 copy-start.61
  46.3 1.5 copy-start.62
  46.3 1.5 copy-start.67
  49.2 6.5 %copy-start.1 = (f32[256,2048]{1,0:T(8,128)}, f32[256,2048]{1,0:T(8,128)S(1)}, u32[]{:S(2)}) copy-start(f32[256,2048]{1,0:T(8,128)S(1)} %fusion.48) | copy-start | bytes 6291460
  49.3 6.4 %collective-permute-start.5 = (f32[256,4]{1,0:T(8,128)S(1)}, f32[256,4]{1,0:T(8,128)S(1)}, u32[]{:S(2)}, u32[]{:S(2)}) collective-permute-start(f32[256,4]{1,0:T(8,128)S(1)} %get-tuple-element.84), channel_id=1, source_target_pairs={{1,0},{2,1},{3,2},{4,3},{5,4},{6,5},{7,6},{8,7},{9,8},{10,9},{11,1... | collective-permute-start | bytes 12296 | tf_op jit(solution)/shard_map/ppermute | solution.py:19
  51.2 5.6 %collective-permute-start.4 = (f32[256,4]{1,0:T(8,128)S(1)}, f32[256,4]{1,0:T(8,128)S(1)}, u32[]{:S(2)}, u32[]{:S(2)}) collective-permute-start(f32[256,4]{1,0:T(8,128)S(1)} %get-tuple-element.85), channel_id=1, source_target_pairs={{0,1},{1,2},{2,3},{3,4},{4,5},{5,6},{6,7},{7,8},{8,9},{9,10},{10,1... | collective-permute-start | bytes 12296 | tf_op jit(solution)/shard_map/ppermute | solution.py:18
  55.6 4.1 %copy-start.22 = (f32[2054]{0:T(1024)S(1)}, f32[2054]{0:T(1024)}, u32[]{:S(2)}) copy-start(f32[2054]{0:T(1024)} %get-tuple-element.48) | copy-start | bytes 24652
  55.6 4.1 %copy-start.23 = (f32[2054]{0:T(1024)S(1)}, f32[2054]{0:T(1024)}, u32[]{:S(2)}) copy-start(f32[2054]{0:T(1024)} %get-tuple-element.49) | copy-start | bytes 24652
  55.7 4.1 %copy-start.24 = (f32[2054]{0:T(1024)S(1)}, f32[2054]{0:T(1024)}, u32[]{:S(2)}) copy-start(f32[2054]{0:T(1024)} %get-tuple-element.57) | copy-start | bytes 24652
  55.7 4.1 %copy-start.44 = (f32[2054]{0:T(1024)S(1)}, f32[2054]{0:T(1024)}, u32[]{:S(2)}) copy-start(f32[2054]{0:T(1024)} %subtract_subtract_fusion.8) | copy-start | bytes 24652
  55.7 4.1 %copy-start.76 = (pred[256]{0:T(512)(128)(4,1)S(1)}, pred[256]{0:T(512)(128)(4,1)}, u32[]{:S(2)}) copy-start(pred[256]{0:T(512)(128)(4,1)} %get-tuple-element.65) | copy-start | bytes 772
  62.9 1.5 copy-start.52
  65.9 7.1 %copy-start = (f32[256,2048]{1,0:T(8,128)}, f32[256,2048]{1,0:T(8,128)S(1)}, u32[]{:S(2)}) copy-start(f32[256,2048]{1,0:T(8,128)S(1)} %fusion.49) | copy-start | bytes 6291460
  66.0 7.0 %collective-permute-start.7 = (f32[256,4]{1,0:T(8,128)S(1)}, f32[256,4]{1,0:T(8,128)S(1)}, u32[]{:S(2)}, u32[]{:S(2)}) collective-permute-start(f32[256,4]{1,0:T(8,128)S(1)} %get-tuple-element.82), channel_id=1, source_target_pairs={{1,0},{2,1},{3,2},{4,3},{5,4},{6,5},{7,6},{8,7},{9,8},{10,9},{11,1... | collective-permute-start | bytes 12296 | tf_op jit(solution)/shard_map/ppermute | solution.py:19
  67.9 6.3 %collective-permute-start.6 = (f32[256,4]{1,0:T(8,128)S(1)}, f32[256,4]{1,0:T(8,128)S(1)}, u32[]{:S(2)}, u32[]{:S(2)}) collective-permute-start(f32[256,4]{1,0:T(8,128)S(1)} %get-tuple-element.83), channel_id=1, source_target_pairs={{0,1},{1,2},{2,3},{3,4},{4,5},{5,6},{6,7},{7,8},{8,9},{9,10},{10,1... | collective-permute-start | bytes 12296 | tf_op jit(solution)/shard_map/ppermute | solution.py:18
  72.6 4.6 %copy-start.13 = (f32[2054]{0:T(1024)S(1)}, f32[2054]{0:T(1024)}, u32[]{:S(2)}) copy-start(f32[2054]{0:T(1024)} %get-tuple-element.45) | copy-start | bytes 24652
  72.6 4.6 %copy-start.14 = (f32[2054]{0:T(1024)S(1)}, f32[2054]{0:T(1024)}, u32[]{:S(2)}) copy-start(f32[2054]{0:T(1024)} %get-tuple-element.46) | copy-start | bytes 24652
  72.6 4.6 %copy-start.15 = (f32[2054]{0:T(1024)S(1)}, f32[2054]{0:T(1024)}, u32[]{:S(2)}) copy-start(f32[2054]{0:T(1024)} %get-tuple-element.59) | copy-start | bytes 24652
  72.6 4.6 %copy-start.43 = (f32[2054]{0:T(1024)S(1)}, f32[2054]{0:T(1024)}, u32[]{:S(2)}) copy-start(f32[2054]{0:T(1024)} %subtract_subtract_fusion.5) | copy-start | bytes 24652
  72.6 4.6 %copy-start.73 = (pred[256]{0:T(512)(128)(4,1)S(1)}, pred[256]{0:T(512)(128)(4,1)}, u32[]{:S(2)}) copy-start(pred[256]{0:T(512)(128)(4,1)} %get-tuple-element.69) | copy-start | bytes 772
  77.2 1.5 copy-start.16
  77.2 1.5 copy-start.17
  77.2 1.5 copy-start.18
  77.2 1.5 copy-start.42
  77.2 1.5 copy-start.72
  80.3 1.5 copy-start.51
  80.3 1.5 copy-start.54
  80.3 1.5 copy-start.55
  80.3 1.5 copy-start.56
  80.4 1.5 copy-start.65
  83.2 7.1 %copy-start.2 = (f32[256,2048]{1,0:T(8,128)}, f32[256,2048]{1,0:T(8,128)S(1)}, u32[]{:S(2)}) copy-start(f32[256,2048]{1,0:T(8,128)S(1)} %fusion.50) | copy-start | bytes 6291460
  83.4 7.0 %collective-permute-start.9 = (f32[256,4]{1,0:T(8,128)S(1)}, f32[256,4]{1,0:T(8,128)S(1)}, u32[]{:S(2)}, u32[]{:S(2)}) collective-permute-start(f32[256,4]{1,0:T(8,128)S(1)} %get-tuple-element.80), channel_id=1, source_target_pairs={{1,0},{2,1},{3,2},{4,3},{5,4},{6,5},{7,6},{8,7},{9,8},{10,9},{11,1... | collective-permute-start | bytes 12296 | tf_op jit(solution)/shard_map/ppermute | solution.py:19
  85.3 6.3 %collective-permute-start.8 = (f32[256,4]{1,0:T(8,128)S(1)}, f32[256,4]{1,0:T(8,128)S(1)}, u32[]{:S(2)}, u32[]{:S(2)}) collective-permute-start(f32[256,4]{1,0:T(8,128)S(1)} %get-tuple-element.81), channel_id=1, source_target_pairs={{0,1},{1,2},{2,3},{3,4},{4,5},{5,6},{6,7},{7,8},{8,9},{9,10},{10,1... | collective-permute-start | bytes 12296 | tf_op jit(solution)/shard_map/ppermute | solution.py:18
  89.9 4.6 %copy-start.4 = (f32[2054]{0:T(1024)S(1)}, f32[2054]{0:T(1024)}, u32[]{:S(2)}) copy-start(f32[2054]{0:T(1024)} %get-tuple-element.41) | copy-start | bytes 24652
  89.9 4.6 %copy-start.5 = (f32[2054]{0:T(1024)S(1)}, f32[2054]{0:T(1024)}, u32[]{:S(2)}) copy-start(f32[2054]{0:T(1024)} %get-tuple-element.42) | copy-start | bytes 24652
  89.9 4.6 %copy-start.6 = (f32[2054]{0:T(1024)S(1)}, f32[2054]{0:T(1024)}, u32[]{:S(2)}) copy-start(f32[2054]{0:T(1024)} %get-tuple-element.43) | copy-start | bytes 24652
  90.0 4.6 %copy-start.41 = (f32[2054]{0:T(1024)S(1)}, f32[2054]{0:T(1024)}, u32[]{:S(2)}) copy-start(f32[2054]{0:T(1024)} %subtract_subtract_fusion.2) | copy-start | bytes 24652
  90.0 4.6 %copy-start.70 = (pred[256]{0:T(512)(128)(4,1)S(1)}, pred[256]{0:T(512)(128)(4,1)}, u32[]{:S(2)}) copy-start(pred[256]{0:T(512)(128)(4,1)} %get-tuple-element.73) | copy-start | bytes 772
  97.7 1.5 copy-start.47
  97.7 1.5 copy-start.48
  97.7 1.5 copy-start.49
  97.7 1.5 copy-start.50
  97.7 1.5 copy-start.63
  97.7 1.5 copy-start.64
  127.6 48.9 %all-to-all-start = ((f32[32,8,2048]{2,1,0:T(8,128)}), f32[32,8,2048]{2,1,0:T(8,128)S(1)}, u32[]{:S(2)}, u32[]{:S(2)}) async-start(f32[32,8,2048]{2,1,0:T(8,128)} %bitcast.25), calls=%async_computation | async-start | bytes 4194304 | tf_op jit(solution)/shard_map/all_to_all | solution.py:104
  (28 other events, 42.2 us)
where the time goes:
time: 180 us; the launch traced here: 179 us
  blocking collectives  68.7 us (38%)
  other arithmetic  35.6 us (20%)
  starting transfers between devices  35.2 us (20%)
  local copies, waits for them, and re-layouts  31.2 us (17%)
  waiting for transfers between devices  4.27 us (2%)
  between operations  4.02 us (2%)
    psum x4, blocking collectives, one_axis_at_a_time(): x = lax.psum(x, axis)  43.3 us
    all_to_all x1, blocking collectives, summed_on_arrival(): tiles = lax.all_to_all(cut_along(x, dim, devices), axis, 0, 0, tiled=True)  25.5 us
    select_n x15, other arithmetic, roll_front(): jnp.where(inside[first_cell:first_cell + cell_count][None, :], rolled, 0.0)  22.2 us
    ppermute x5, starting transfers between devices, extended(): before = lax.ppermute(last, axis, up)  19.9 us
    concatenate x5, local copies, waits for them, and re-layouts, extended(): x = jnp.concatenate([before, x, after], axis=dim)  12.3 us
    ppermute x5, starting transfers between devices, extended(): after = lax.ppermute(leading, axis, down)  11 us
    sub x14, other arithmetic, roll_once(): middle = 1.0 - prob_up - prob_down  7.8 us
    slice x9, local copies, waits for them, and re-layouts, roll_front(): rolled = roll_once(padded, coefs[0], coefs[1], coefs[2])  7.13 us
  transfers between devices with their start and end apart: 11, of which 5 were waited for; matrix products, arithmetic and copies ran while one was open for 15% of the time, Pallas kernels for 0%

commit v1 on v0

v1 whole, which is shorter than its diff:
```python
import functools

import jax
import jax.numpy as jnp
from jax import lax
from jax.experimental import pallas as pl
from jax.experimental.pallas import tpu as pltpu
from jax.sharding import Mesh
from jax.sharding import PartitionSpec as P

LANES = 128
ROWS = 8
OFF = 1e30
TRADE = ("trade_0", "trade_1")
NODE = ("x_0", "x_1", "y_0", "y_1", "core")
TRADE_NODE = TRADE + NODE


def scaled_rows(up, down, disc, ann):
    row = lax.broadcasted_iota(jnp.int32, ann.shape, 0)
    width = ann.shape[1]
    before = jnp.where(row == 0, 1.0, pltpu.roll(ann, 1, 0))
    share = disc / ann
    a = share * up * pltpu.roll(before, width - 1, 1)
    b = share * (1.0 - up - down) * before
    c = share * down * pltpu.roll(before, 1, 1)
    return a, b, c


def trade_columns(ex_ref, bucket_ref, sign_ref, table_ref, half):
    ex = ex_ref[:, half * LANES : (half + 1) * LANES]
    bits = jnp.left_shift(jnp.ones_like(ex), ex)
    mask = bits[0:1] | bits[1:2] | bits[2:3] | bits[3:4]
    bucket = bucket_ref[half : half + 1, :]
    levels = lax.broadcasted_iota(jnp.int32, (table_ref.shape[1], LANES), 0)
    strike = jnp.dot(
        table_ref[...],
        (levels == bucket).astype(jnp.float32),
        precision=lax.Precision.HIGHEST,
        preferred_element_type=jnp.float32,
    )
    sign = (2 * sign_ref[half : half + 1, :] - 1).astype(jnp.float32)

    def column(r):
        return jnp.transpose(jnp.broadcast_to(r, (LANES, LANES)))

    return column(sign), column(sign * strike), column(mask.astype(jnp.float32)).astype(jnp.int32)


def on_terms(sign, key, mask, step):
    on = (mask & (1 << step)) != 0
    return jnp.where(on, sign, 0.0), jnp.where(on, key, OFF)


def pack_kernel(v_ref, up_ref, dn_ref, dc_ref, sr_ref, an_ref, sp_ref, out_ref):
    n, steps = v_ref.shape[0], up_ref.shape[0]
    out_ref[0:n, :] = v_ref[...]
    for i, ref in enumerate((up_ref, dn_ref, dc_ref, sr_ref, an_ref)):
        out_ref[n + i * steps : n + (i + 1) * steps, :] = ref[...]
    out_ref[n + 5 * steps : n + 5 * steps + ROWS, :] = jnp.broadcast_to(sp_ref[0:1, :], (ROWS, LANES))


def interior_kernel(
    groups, v_ref, up_ref, dn_ref, dc_ref, sr_ref, an_ref, sp_ref, ex_ref, bk_ref, sg_ref, tb_ref,
    out_ref, acc_ref, sgn_out, key_out, mask_out,
    nat_ref, coef_ref, x_ref, node_ref, buf_ref,
):
    steps, width = up_ref.shape
    tiles = width // LANES
    block = v_ref.shape[0]
    rows = groups * ROWS
    i = pl.program_id(0)

    def spread(src, dst, count):
        for t in range(tiles):
            node_ref[t * LANES : (t + 1) * LANES, 0:count] = jnp.transpose(
                src[0:count, t * LANES : (t + 1) * LANES]
            )
        for k in range(tiles):
            dst[0:count, k * LANES : (k + 1) * LANES] = jnp.transpose(
                node_ref[pl.ds(k, LANES, stride=tiles), 0:count]
            )

    @pl.when(i == 0)
    def _():
        a, b, c = scaled_rows(up_ref[...], dn_ref[...], dc_ref[...], an_ref[...])
        for j, z in enumerate((a, b, c, sr_ref[...])):
            nat_ref[j * steps : (j + 1) * steps, :] = z
        nat_ref[4 * steps : 4 * steps + ROWS, :] = an_ref[steps - ROWS : steps, :]
        for t in range(tiles):
            nat_ref[4 * steps + ROWS : 4 * steps + 2 * ROWS, t * LANES : (t + 1) * LANES] = jnp.broadcast_to(
                sp_ref[t : t + 1, :], (ROWS, LANES)
            )
        nat_ref[4 * steps + 2 * ROWS :, :] = jnp.zeros((LANES - 4 * steps - 2 * ROWS, width), jnp.float32)
        spread(nat_ref, coef_ref, LANES)
        for half in range(2):
            sign, key, mask = trade_columns(ex_ref, bk_ref, sg_ref, tb_ref, half)
            at = pl.ds(half * LANES, LANES)
            sgn_out[at, :] = sign
            key_out[at, :] = key
            mask_out[at, :] = mask

    spread(v_ref, x_ref, block)
    lane = lax.broadcasted_iota(jnp.int32, (ROWS, LANES), 1)
    own = (lane > 0) & (lane < LANES - 1)

    @pl.loop(0, block // rows)
    def _(g):
        at = [pl.ds(pl.multiple_of(g * rows + ROWS * q, ROWS), ROWS) for q in range(groups)]
        base = [pl.ds(pl.multiple_of(i * block + g * rows + ROWS * q, ROWS), ROWS) for q in range(groups)]
        sign = [sgn_out[z, :] for z in base]
        key = [key_out[z, :] for z in base]
        mask = [mask_out[z, :] for z in base]

        def wide(r, k):
            return jnp.broadcast_to(coef_ref[r : r + 1, k * LANES : (k + 1) * LANES], (ROWS, LANES))

        def load(s, q, k):
            cols = slice(k * LANES, (k + 1) * LANES)
            return x_ref[at[q], cols] if s == 0 else buf_ref[(s - 1) % 2, ROWS * q : ROWS * (q + 1), cols]

        acc = [jnp.zeros((ROWS, LANES), jnp.float32)] * groups
        ends = [[load(0, q, 0), load(0, q, tiles - 1)] for q in range(groups)]
        for s in range(steps):
            terms = [on_terms(sign[q], key[q], mask[q], s) for q in range(groups)]
            up = [pltpu.roll(ends[q][0], LANES - 1, 1) for q in range(groups)]
            dn = [pltpu.roll(ends[q][1], 1, 1) for q in range(groups)]
            mid, nxt = [None] * groups, [None] * groups
            for k in [tiles - 1] + list(range(tiles - 1)):
                a, b, c, p = (wide(j * steps + s, k) for j in range(4))
                if s == steps - 1:
                    fin, price = wide(4 * steps + ROWS - 1, k), wide(4 * steps + ROWS, k)
                for q in range(groups):
                    if k == tiles - 1:
                        below, here, above = load(s, q, k - 1), load(s, q, k), up[q]
                    elif k == 0:
                        below, here, above = dn[q], load(s, q, 0), load(s, q, 1)
                        mid[q], nxt[q] = here, above
                    else:
                        below, here, above = mid[q], nxt[q], load(s, q, k + 1)
                        mid[q], nxt[q] = here, above
                    alpha, beta = terms[q]
                    new = jnp.maximum(a * above + b * here + c * below, alpha * p - beta)
                    cols = slice(k * LANES, (k + 1) * LANES)
                    if s == steps - 1:
                        new = new * fin
                        x_ref[at[q], cols] = new
                        acc[q] = acc[q] + new * price
                    else:
                        buf_ref[s % 2, ROWS * q : ROWS * (q + 1), cols] = new
                    if k == 0:
                        ends[q][0] = new
                    if k == tiles - 1:
                        ends[q][1] = new
        for q in range(groups):
            acc_ref[at[q], :] = jnp.where(own, acc[q], 0.0)

    for k in range(tiles):
        node_ref[pl.ds(k, LANES, stride=tiles), 0:block] = jnp.transpose(
            x_ref[:, k * LANES : (k + 1) * LANES]
        )
    for t in range(tiles):
        out_ref[:, t * LANES : (t + 1) * LANES] = jnp.transpose(
            node_ref[t * LANES : (t + 1) * LANES, 0:block]
        )


def edge_kernel(
    far_ref, halo_ref, v_ref, up_ref, dn_ref, dc_ref, sr_ref, an_ref, sp_ref, sgn_ref, key_ref, mask_ref,
    acc_ref, old_ref, out_ref, price_ref, e_ref, p_ref,
):
    n, steps = v_ref.shape[0], up_ref.shape[0]
    i = pl.program_id(0)
    lane = lax.broadcasted_iota(jnp.int32, (ROWS, LANES), 1)

    @pl.when(i == 0)
    def _():
        far = far_ref[0]

        def joined(at, ref):
            mine = ref[...]
            beyond = halo_ref[n + at : n + at + mine.shape[0], :]
            here = lax.broadcasted_iota(jnp.int32, mine.shape, 1)
            return jnp.where(here < LANES // 2, beyond, mine)

        up, dn, dc, sr, an = (
            joined(j * steps, ref) for j, ref in enumerate((up_ref, dn_ref, dc_ref, sr_ref, an_ref))
        )
        price = jnp.where(lane < LANES // 2, halo_ref[n + 5 * steps : n + 5 * steps + ROWS, :], jnp.broadcast_to(sp_ref[sp_ref.shape[0] - 1 :, :], (ROWS, LANES)))
        price = jnp.where((lane < steps) | (lane >= LANES - steps), price, 0.0)
        a, b, c = scaled_rows(up, dn, dc, an)
        rim = lax.broadcasted_iota(jnp.int32, a.shape, 1)
        a = jnp.where((rim == LANES - 1) & (far == 1), 0.0, a)
        c = jnp.where((rim == 0) & (far == 1), 0.0, c)
        for half in range(2):
            at = [slice(half * LANES + q * ROWS, half * LANES + (q + 1) * ROWS) for q in range(LANES // ROWS)]
            x = [jnp.where(lane < LANES // 2, halo_ref[z, :], v_ref[z, :]) for z in at]
            sign, key, mask = ([ref[z, :] for z in at] for ref in (sgn_ref, key_ref, mask_ref))
            for s in range(steps):
                above = [pltpu.roll(z, LANES - 1, 1) for z in x]
                below = [pltpu.roll(z, 1, 1) for z in x]
                ra, rb, rc, rp = (jnp.broadcast_to(z[s : s + 1, :], (ROWS, LANES)) for z in (a, b, c, sr))
                for q in range(len(x)):
                    alpha, beta = on_terms(sign[q], key[q], mask[q], s)
                    x[q] = jnp.maximum(ra * above[q] + rb * x[q] + rc * below[q], alpha * rp - beta)
            fin = jnp.broadcast_to(an[steps - 1 : steps, :], (ROWS, LANES))
            for q, z in enumerate(at):
                e = x[q] * fin
                e_ref[z, :] = e
                p_ref[z, :] = acc_ref[z, :] + e * price
        for half in range(2):
            part = jnp.transpose(p_ref[half * LANES : (half + 1) * LANES, :])
            price_ref[half : half + 1, :] = jnp.sum(part, axis=0, keepdims=True)

    side = lax.broadcasted_iota(jnp.int32, (n, LANES), 1)

    @pl.when(i == 0)
    def _():
        out_ref[...] = jnp.where(side < steps, e_ref[...], old_ref[...])

    @pl.when(i == 1)
    def _():
        out_ref[...] = jnp.where(side >= LANES - steps, e_ref[...], old_ref[...])


def whole(shape):
    return pl.BlockSpec(shape, lambda i: (0,) * len(shape))


def vmem_scratch(shape):
    return pltpu.VMEM(shape, jnp.float32)


def local(values_in, prob_up, prob_down, discount, swap_rate, annuity, state_price, exercise_step, strike_bucket, notional_sign, strike_table):
    n, width = values_in.shape
    steps = prob_up.shape[0]
    node_count = lax.axis_size(NODE)
    tiles = width // LANES
    table = (prob_up, prob_down, discount, swap_rate, annuity)
    price_rows = state_price.reshape(tiles, LANES)
    trades = (exercise_step.T, strike_bucket.reshape(-1, LANES), notional_sign.reshape(-1, LANES), strike_table.reshape(1, -1))
    f32 = jnp.float32

    halo_rows = n + 5 * steps + ROWS
    packed = pl.pallas_call(
        pack_kernel,
        grid=(1,),
        in_specs=[whole((n, LANES))] + [whole((steps, LANES))] * 5 + [whole(price_rows.shape)],
        out_specs=whole((halo_rows, LANES)),
        out_shape=jax.ShapeDtypeStruct((halo_rows, LANES), f32),
        name="pack",
    )(values_in, *table, price_rows)
    halo = lax.ppermute(packed, NODE, [((i + 1) % node_count, i) for i in range(node_count)])

    block = LANES
    side = jax.ShapeDtypeStruct((n, LANES), f32)
    rolled, acc, sign, key, mask = pl.pallas_call(
        functools.partial(interior_kernel, 4),
        grid=(n // block,),
        in_specs=[pl.BlockSpec((block, width), lambda i: (i, 0))]
        + [whole((steps, width))] * 5
        + [whole(z.shape) for z in (price_rows,) + trades],
        out_specs=[
            pl.BlockSpec((block, width), lambda i: (i, 0)),
            pl.BlockSpec((block, LANES), lambda i: (i, 0)),
        ]
        + [whole((n, LANES))] * 3,
        out_shape=[jax.ShapeDtypeStruct((n, width), f32), side, side, side, jax.ShapeDtypeStruct((n, LANES), jnp.int32)],
        scratch_shapes=[
            vmem_scratch((LANES, width)),
            vmem_scratch((LANES, width)),
            vmem_scratch((block, width)),
            vmem_scratch((width, LANES)),
            vmem_scratch((2, 4 * ROWS, width)),
        ],
        cost_estimate=pl.CostEstimate(flops=12 * n * width * steps, bytes_accessed=3 * 8 * n * width, transcendentals=0),
        name="interior",
    )(values_in, *table, price_rows, *trades)

    far = (lax.axis_index(NODE) == node_count - 1).astype(jnp.int32).reshape(1)
    last_tile = lambda i: (0, tiles - 1)
    ends = pl.BlockSpec((n, LANES), lambda i: (0, i * (tiles - 1)))
    rolled, partial = pl.pallas_call(
        edge_kernel,
        grid=(2,),
        in_specs=[
            pl.BlockSpec(memory_space=pltpu.SMEM),
            whole((halo_rows, LANES)),
            pl.BlockSpec((n, LANES), last_tile),
        ]
        + [pl.BlockSpec((steps, LANES), last_tile)] * 5
        + [whole(price_rows.shape)]
        + [whole((n, LANES))] * 4
        + [ends],
        out_specs=[ends, whole((n // LANES, LANES))],
        out_shape=[jax.ShapeDtypeStruct((n, width), f32), jax.ShapeDtypeStruct((n // LANES, LANES), f32)],
        scratch_shapes=[vmem_scratch((n, LANES)), vmem_scratch((n, LANES))],
        input_output_aliases={13: 0},
        name="edge",
    )(far, halo, values_in, *table, price_rows, sign, key, mask, acc, rolled)

    rows = n // node_count
    moved = lax.all_to_all(rolled.reshape(node_count, rows, width), NODE, 0, 0, tiled=True)
    for axis in reversed(NODE):
        partial = lax.psum(partial, axis)
    mine = lax.dynamic_slice_in_dim(partial.reshape(node_count, rows), lax.axis_index(NODE), 1, 0)
    prices = mine.reshape(rows)
    total = jnp.sum(partial)
    for axis in reversed(TRADE):
        total = lax.psum(total, axis)

    flat = jnp.swapaxes(moved, 0, 1).reshape(rows, node_count * width)
    shifted = jnp.roll(flat, width, axis=1)
    column = lax.broadcasted_iota(jnp.int32, (1, node_count * width), 1)
    values = jnp.where(column % width < steps, shifted, flat)
    return values, prices, total / n


def solution(mesh):
    split = Mesh(mesh.devices.reshape(2, 2, 2, 2, 2, 2, 2), TRADE_NODE)
    in_specs = (
        P(TRADE, NODE),
        P(None, NODE),
        P(None, NODE),
        P(None, NODE),
        P(None, NODE),
        P(None, NODE),
        P(NODE),
        P(TRADE, None),
        P(TRADE),
        P(TRADE),
        P(),
    )
    out_specs = (P(TRADE_NODE, None), P(TRADE_NODE), P())
    return jax.shard_map(local, mesh=split, in_specs=in_specs, out_specs=out_specs, check_vma=False)
```

time: 180 us -> 93.9 us (0.52)
  the two profiles are of different devices: /device:TPU:1 before, /device:TPU:6 now
where the time goes in v1:
time: 93.9 us; the launch traced here: 93.5 us
  blocking collectives  55.7 us (59%)
  Pallas kernels  22.7 us (24%)
  starting transfers between devices  8.96 us (10%)
  between operations  2.48 us (3%)
  other arithmetic  2.28 us (2%)
  local copies, waits for them, and re-layouts  1.4 us (1%)
    psum x5, blocking collectives, local(): partial = lax.psum(partial, axis)  42.8 us
    pallas_call x1, Pallas kernels, local(): pl.pallas_call(functools.partial(interior_kernel, 4), grid=(n // block,),...  17.2 us
    psum x2, blocking collectives, local(): total = lax.psum(total, axis)  12.9 us
    all_to_all x1, starting transfers between devices, local(): lax.all_to_all(rolled.reshape(node_count, rows, width), NODE, 0, 0, tiled...  6.24 us
    pallas_call x1, Pallas kernels, local(): pl.pallas_call(edge_kernel, grid=(2,), in_specs=[pl.BlockSpec(memory_spac...  3.78 us
    ppermute x1, starting transfers between devices, local(): lax.ppermute(packed, NODE, [((i + 1) % node_count, i) for i in range(node...  2.72 us
  transfers between devices with their start and end apart: 2, of which 0 were waited for; matrix products, arithmetic and copies ran while one was open for 1% of the time, Pallas kernels for 18%

profile of v1, /device:TPU:6, one launch (start us, length us, event | category | flops | bytes accessed | tf_op | source)
XLA Modules:
  0.0 93.5 jit_solution(1980621055729751722)
XLA Ops:
  0.6 1.6 %pack.1 = f32[344,128]{1,0:T(8,128)} custom-call(f32[256,2048]{1,0:T(8,128)} %v_ref.5, f32[16,2048]{1,0:T(8,128)} %up_ref.5, f32[16,2048]{1,0:T(8,128)} %dn_ref.5, f32[16,2048]{1,0:T(8,128)} %dc_ref.5, f32[16,2048]{1,0:T(8,128)} %sr_ref.5, f32[16,2048]{1,0:T(8,128)} %an_ref.5, f32[16,128]{1,0:T(8,128)} %bitcast.16), custom_call_target="tpu_custom_call" | custom-call | tf_op jit(solution)/shard_map/pack/pallas_call | solution.py:245
  2.3 2.7 %collective-permute-start = (f32[344,128]{1,0:T(8,128)}, f32[344,128]{1,0:T(8,128)S(1)}, u32[]{:S(2)}, u32[]{:S(2)}) collective-permute-start(f32[344,128]{1,0:T(8,128)} %pack.1), channel_id=1, source_target_pairs={{1,0},{2,1},{3,2},{4,3},{5,4},{6,5},{7,6},{8,7},{9,8},{10,9},{11,1... | collective-permute-start | bytes 528392 | tf_op jit(solution)/shard_map/ppermute | solution.py:253
  5.0 17.2 %interior.1 = (f32[256,2048]{1,0:T(8,128)}, f32[256,128]{1,0:T(8,128)}, f32[256,128]{1,0:T(8,128)}, f32[256,128]{1,0:T(8,128)}, s32[256,128]{1,0:T(8,128)}) custom-call(f32[256,2048]{1,0:T(8,128)} %v_ref.5, f32[16,2048]{1,0:T(8,128)} %up_ref.5, f32[16,2048]{1,0:T(8,128)} %dn_ref.5, f32[16,2048]{1,0:T(8,128)} %dc_ref.5, f32[16,2048]{1,0:T(8,128)} %sr_ref.5, ...), custom_call_target="tpu_custom_call" | custom-call | flops 100663296 | bytes 12582912 | tf_op jit(solution)/shard_map/interior/pallas_call | solution.py:257
  22.2 0.0 collective-permute-done.halo_ref
  22.2 0.0 copy-start
  22.2 0.7 copy-done
  22.9 3.8 %edge.1 = (f32[256,2048]{1,0:T(8,128)}, f32[2,128]{1,0:T(2,128)}) custom-call(s32[1]{0:T(128)} %bitcast.far_ref, f32[344,128]{1,0:T(8,128)} %copy-done, f32[256,2048]{1,0:T(8,128)} %v_ref.5, f32[16,2048]{1,0:T(8,128)} %up_ref.5, f32[16,2048]{1,0:T(8,128)} %dn_ref.5, f32[16,2048]{1,0:T(8,128)} %dc_ref.5, ...), custom_call_target="tpu_custom_call", output_to_operand_aliasing={{0}: (13, {})} | custom-call | tf_op jit(solution)/shard_map/edge/pallas_call | solution.py:283
  26.7 0.0 copy-start.1
  26.7 6.2 %all-to-all-start = ((f32[32,8,2048]{2,1,0:T(8,128)}), f32[32,8,2048]{2,1,0:T(8,128)S(1)}, u32[]{:S(2)}, u32[]{:S(2)}) async-start(f32[32,8,2048]{2,1,0:T(8,128)} %bitcast.15), calls=%async_computation | async-start | bytes 4194304 | tf_op jit(solution)/shard_map/all_to_all | solution.py:303
  33.0 0.0 copy-done.1
  33.0 2.5 %psum.49 = f32[2,128]{1,0:T(2,128)S(1)} all-reduce(f32[2,128]{1,0:T(2,128)S(1)} %copy-done.1), channel_id=1, replica_groups=mesh['trade_0'=2,'trade_1'=2,'x_0'=2,'x_1'=2,'y_0'=2,'y_1'=2,'core'=2] {..., use_global_device_ids=true, to_apply=%region_0.0 | all-reduce | flops 256 | bytes 2048 | tf_op jit(solution)/shard_map/psum | solution.py:305
  35.4 22.6 %psum.50 = f32[2,128]{1,0:T(2,128)S(1)} all-reduce(f32[2,128]{1,0:T(2,128)S(1)} %psum.49), channel_id=1, replica_groups=mesh['trade_0'=2,'trade_1'=2,'x_0'=2,'x_1'=2,'y_0'=2,'y_1'=2,'core'=2] {..., use_global_device_ids=true, to_apply=%region_1.0 | all-reduce | flops 256 | bytes 2048 | tf_op jit(solution)/shard_map/psum | solution.py:305
  58.0 6.4 %psum.51 = f32[2,128]{1,0:T(2,128)S(1)} all-reduce(f32[2,128]{1,0:T(2,128)S(1)} %psum.50), channel_id=1, replica_groups=mesh['trade_0'=2,'trade_1'=2,'x_0'=2,'x_1'=2,'y_0'=2,'y_1'=2,'core'=2] {..., use_global_device_ids=true, to_apply=%region_2.0 | all-reduce | flops 256 | bytes 2048 | tf_op jit(solution)/shard_map/psum | solution.py:305
  64.4 4.9 %psum.52 = f32[2,128]{1,0:T(2,128)S(1)} all-reduce(f32[2,128]{1,0:T(2,128)S(1)} %psum.51), channel_id=1, replica_groups=mesh['trade_0'=2,'trade_1'=2,'x_0'=2,'x_1'=2,'y_0'=2,'y_1'=2,'core'=2] {..., use_global_device_ids=true, to_apply=%region_3.0 | all-reduce | flops 256 | bytes 2048 | tf_op jit(solution)/shard_map/psum | solution.py:305
  69.4 6.4 %psum.53 = f32[2,128]{1,0:T(2,128)S(1)} all-reduce(f32[2,128]{1,0:T(2,128)S(1)} %psum.52), channel_id=1, replica_groups=mesh['trade_0'=2,'trade_1'=2,'x_0'=2,'x_1'=2,'y_0'=2,'y_1'=2,'core'=2] {..., use_global_device_ids=true, to_apply=%region_4.0 | all-reduce | flops 256 | bytes 2048 | tf_op jit(solution)/shard_map/psum | solution.py:305
  75.8 0.6 reduce_sum.9
  76.4 5.5 %psum.54 = f32[]{:T(128)} all-reduce(f32[]{:T(128)} %reduce_sum.9), channel_id=1, replica_groups=mesh['trade_0'=2,'trade_1'=2,'x_0'=2,'x_1'=2,'y_0'=2,'y_1'=2,'core'=2] {..., use_global_device_ids=true, to_apply=%region_6.0 | all-reduce | flops 1 | bytes 8 | tf_op jit(solution)/shard_map/psum | solution.py:310
  81.9 7.4 %psum.55 = f32[]{:T(128)} all-reduce(f32[]{:T(128)} %psum.54), channel_id=1, replica_groups=mesh['trade_0'=2,'trade_1'=2,'x_0'=2,'x_1'=2,'y_0'=2,'y_1'=2,'core'=2] {..., use_global_device_ids=true, to_apply=%region_7.0 | all-reduce | flops 1 | bytes 8 | tf_op jit(solution)/shard_map/psum | solution.py:310
  89.3 0.1 reshape.60
  90.1 0.5 dynamic-slice_bitcast_fusion
  90.6 0.0 all-to-all-done
  90.6 0.1 slice.11
  90.7 1.6 %maximum_select_fusion = f32[8,65536]{1,0:T(8,128)} fusion(f32[8,65536]{1,0:T(8,128)S(1)} %bitcast.14, f32[8,63488]{1,0:T(8,128)S(1)} %slice.11, f32[8,2048]{1,0:T(8,128)S(1)} %slice.10, pred[65536]{0:T(1024)(128)(4,1)S(1)} %fusion), kind=kLoop, calls=%fused_computation | loop fusion | flops 1048576 | bytes 6356992 | tf_op jit(solution)/shard_map/jit(_where)/select_n | solution.py:315
  (2 shorter events, 0.0 us)
Async XLA Ops:
  2.3 20.0 %collective-permute-start = (f32[344,128]{1,0:T(8,128)}, f32[344,128]{1,0:T(8,128)S(1)}, u32[]{:S(2)}, u32[]{:S(2)}) collective-permute-start(f32[344,128]{1,0:T(8,128)} %pack.1), channel_id=1, source_target_pairs={{1,0},{2,1},{3,2},{4,3},{5,4},{6,5},{7,6},{8,7},{9,8},{10,9},{11,1... | collective-permute-start | bytes 528392 | tf_op jit(solution)/shard_map/ppermute | solution.py:253
  22.2 0.7 copy-start
  26.7 6.3 %copy-start.1 = (f32[2,128]{1,0:T(2,128)S(1)}, f32[2,128]{1,0:T(2,128)}, u32[]{:S(2)}) copy-start(f32[2,128]{1,0:T(2,128)} %get-tuple-element.16) | copy-start | bytes 3076
  26.7 63.9 %all-to-all-start = ((f32[32,8,2048]{2,1,0:T(8,128)}), f32[32,8,2048]{2,1,0:T(8,128)S(1)}, u32[]{:S(2)}, u32[]{:S(2)}) async-start(f32[32,8,2048]{2,1,0:T(8,128)} %bitcast.15), calls=%async_computation | async-start | bytes 4194304 | tf_op jit(solution)/shard_map/all_to_all | solution.py:303

commit v2 on v1

v2 whole, which is shorter than its diff:
```python
import functools

import jax
import jax.numpy as jnp
from jax import lax
from jax.experimental import pallas as pl
from jax.experimental.pallas import tpu as pltpu
from jax.sharding import Mesh
from jax.sharding import PartitionSpec as P

LANES = 128
HALF = LANES // 2
ROWS = 8
CHUNKS = 2
TOGETHER = 4
OFF = 1e30
NODE = ("node_0", "node_1", "node_2")
TRADE_NODE = ("trade",) + NODE


def scaled_rows(up, down, disc, ann):
    row = lax.broadcasted_iota(jnp.int32, ann.shape, 0)
    width = ann.shape[1]
    before = jnp.where(row == 0, 1.0, pltpu.roll(ann, 1, 0))
    share = disc / ann
    a = share * up * pltpu.roll(before, width - 1, 1)
    b = share * (1.0 - up - down) * before
    c = share * down * pltpu.roll(before, 1, 1)
    return a, b, c


def trade_columns(ex_ref, bucket_ref, sign_ref, table_ref, half):
    ex = ex_ref[:, half * LANES : (half + 1) * LANES]
    bits = jnp.left_shift(jnp.ones_like(ex), ex)
    mask = bits[0:1] | bits[1:2] | bits[2:3] | bits[3:4]
    bucket = bucket_ref[half : half + 1, :]
    levels = lax.broadcasted_iota(jnp.int32, (table_ref.shape[1], LANES), 0)
    strike = jnp.dot(
        table_ref[...],
        (levels == bucket).astype(jnp.float32),
        precision=lax.Precision.HIGHEST,
        preferred_element_type=jnp.float32,
    )
    sign = (2 * sign_ref[half : half + 1, :] - 1).astype(jnp.float32)

    def column(r):
        return jnp.transpose(jnp.broadcast_to(r, (LANES, LANES)))

    return column(sign), column(sign * strike), column(mask.astype(jnp.float32)).astype(jnp.int32)


def on_terms(sign, key, mask, step):
    on = (mask & (1 << step)) != 0
    return jnp.where(on, sign, 0.0), jnp.where(on, key, OFF)


def pack_kernel(v_ref, up_ref, dn_ref, dc_ref, sr_ref, an_ref, sp_ref, out_ref):
    n, steps = v_ref.shape[0], up_ref.shape[0]
    out_ref[0:n, :] = v_ref[...]
    for i, ref in enumerate((up_ref, dn_ref, dc_ref, sr_ref, an_ref)):
        out_ref[n + i * steps : n + (i + 1) * steps, :] = ref[...]
    out_ref[n + 5 * steps : n + 5 * steps + ROWS, :] = jnp.broadcast_to(sp_ref[0:1, :], (ROWS, LANES))


def roll_kernel(
    last, far_ref, v_ref, up_ref, dn_ref, dc_ref, sr_ref, an_ref, sp_ref,
    v2_ref, up2_ref, dn2_ref, dc2_ref, sr2_ref, an2_ref, sp2_ref,
    ex_ref, bk_ref, sg_ref, tb_ref, *rest,
):
    if last:
        before_ref, out_ref, sum_ref = rest[:3]
    else:
        out_ref, sum_ref = rest[:2]
    nat_ref, coef_ref, strip_ref, x_ref, node_ref, buf_ref, rim_ref, e_ref, sgn_ref, key_ref, mask_ref = rest[2 + last :]
    steps, width = up_ref.shape
    tiles = width // LANES
    block = v_ref.shape[0]
    groups = block // ROWS
    spoiled = steps // tiles
    i = pl.program_id(0)
    lane = lax.broadcasted_iota(jnp.int32, (ROWS, LANES), 1)

    def cols(k):
        return slice(k * LANES, (k + 1) * LANES)

    def rows(q):
        return slice(q * ROWS, (q + 1) * ROWS)

    def spread(src, dst):
        for t in range(tiles):
            node_ref[cols(t), :] = jnp.transpose(src[:, cols(t)])
        for k in range(tiles):
            dst[:, cols(k)] = jnp.transpose(node_ref[pl.ds(k, LANES, stride=tiles), :])

    @pl.when(i == 0)
    def _():
        a, b, c = scaled_rows(up_ref[...], dn_ref[...], dc_ref[...], an_ref[...])
        for j, z in enumerate((a, b, c, sr_ref[...])):
            nat_ref[j * steps : (j + 1) * steps, :] = z
        nat_ref[4 * steps : 4 * steps + ROWS, :] = an_ref[steps - ROWS : steps, :]
        for t in range(tiles):
            nat_ref[4 * steps + ROWS : 4 * steps + 2 * ROWS, cols(t)] = jnp.broadcast_to(
                sp_ref[t : t + 1, :], (ROWS, LANES)
            )
        nat_ref[4 * steps + 2 * ROWS :, :] = jnp.zeros((LANES - 4 * steps - 2 * ROWS, width), jnp.float32)
        spread(nat_ref, coef_ref)

        side = lax.broadcasted_iota(jnp.int32, (steps, LANES), 1)

        def joined(ref, beyond):
            return jnp.where(side < HALF, beyond[...], ref[:, width - LANES :])

        an = joined(an_ref, an2_ref)
        a, b, c = scaled_rows(joined(up_ref, up2_ref), joined(dn_ref, dn2_ref), joined(dc_ref, dc2_ref), an)
        far = far_ref[0] == 1
        a = jnp.where((side == LANES - 1) & far, 0.0, a)
        c = jnp.where((side == 0) & far, 0.0, c)
        for j, z in enumerate((a, b, c, joined(sr_ref, sr2_ref))):
            strip_ref[j * steps : (j + 1) * steps, :] = z
        strip_ref[4 * steps : 4 * steps + ROWS, :] = an[steps - ROWS : steps, :]
        price = jnp.where(lane < HALF, sp2_ref[0:1, :], sp_ref[tiles - 1 : tiles, :])
        strip_ref[4 * steps + ROWS : 4 * steps + 2 * ROWS, :] = jnp.where(
            (lane < steps) | (lane >= LANES - steps), price, 0.0
        )
        for half in range(sgn_ref.shape[0] // LANES):
            sign, key, mask = trade_columns(ex_ref, bk_ref, sg_ref, tb_ref, half)
            at = pl.ds(half * LANES, LANES)
            sgn_ref[at, :] = sign
            key_ref[at, :] = key
            mask_ref[at, :] = mask
        if last:
            sum_ref[...] = jnp.zeros((ROWS, LANES), jnp.float32)

    spread(v_ref, x_ref)
    base = [pl.ds(pl.multiple_of(i * block + ROWS * q, ROWS), ROWS) for q in range(groups)]

    def wide(ref, r, at):
        return jnp.broadcast_to(ref[r : r + 1, at], (ROWS, LANES))

    def load(s, q, k):
        return x_ref[rows(q), cols(k)] if s == 0 else buf_ref[(s - 1) % 2, rows(q), cols(k)]

    def put_rim(s, q, first, final):
        rim_ref[s % 2, 0, rows(q), :] = pltpu.roll(first, LANES - 1, 1)
        rim_ref[s % 2, 1, rows(q), :] = pltpu.roll(final, 1, 1)

    def put_strip(s, q, e):
        e_ref[s % 2, 0, rows(q), :] = e
        e_ref[s % 2, 1, rows(q), :] = pltpu.roll(e, LANES - 1, 1)
        e_ref[s % 2, 2, rows(q), :] = pltpu.roll(e, 1, 1)

    for q in range(groups):
        put_rim(1, q, load(0, q, 0), load(0, q, tiles - 1))
        put_strip(1, q, jnp.where(lane < HALF, v2_ref[rows(q), :], v_ref[rows(q), width - LANES :]))
    acc = [None] * groups
    for s in range(steps):
        done = s == steps - 1
        for q0 in range(0, groups, TOGETHER):
            qs = range(q0, q0 + TOGETHER)
            terms = {q: on_terms(sgn_ref[base[q], :], key_ref[base[q], :], mask_ref[base[q], :], s) for q in qs}
            a, b, c, p = (wide(strip_ref, j * steps + s, slice(None)) for j in range(4))
            for q in qs:
                alpha, beta = terms[q]
                z = (s + 1) % 2
                e = a * e_ref[z, 1, rows(q), :] + b * e_ref[z, 0, rows(q), :] + c * e_ref[z, 2, rows(q), :]
                e = jnp.maximum(e, alpha * p - beta)
                if done:
                    e = e * strip_ref[4 * steps + ROWS - 1 : 4 * steps + ROWS, :]
                    e_ref[s % 2, 0, rows(q), :] = e
                    acc[q] = e * strip_ref[4 * steps + ROWS : 4 * steps + 2 * ROWS, :]
                else:
                    put_strip(s, q, e)
            below = {q: rim_ref[(s + 1) % 2, 1, rows(q), :] for q in qs}
            here = {q: load(s, q, 0) for q in qs}
            inner = {q: None for q in qs}
            first = {}
            for k in range(tiles):
                a, b, c, p = (wide(coef_ref, j * steps + s, cols(k)) for j in range(4))
                if done:
                    fin = wide(coef_ref, 4 * steps + ROWS - 1, cols(k))
                    price = wide(coef_ref, 4 * steps + ROWS, cols(k))
                for q in qs:
                    above = load(s, q, k + 1) if k + 1 < tiles else rim_ref[(s + 1) % 2, 0, rows(q), :]
                    alpha, beta = terms[q]
                    new = jnp.maximum(a * above + b * here[q] + c * below[q], alpha * p - beta)
                    below[q], here[q] = here[q], above
                    if done:
                        new = new * fin
                        x_ref[rows(q), cols(k)] = new
                        inner[q] = new * price if k == 0 else inner[q] + new * price
                    else:
                        buf_ref[s % 2, rows(q), cols(k)] = new
                        if k == 0:
                            first[q] = new
                        if k == tiles - 1:
                            put_rim(s, q, first[q], new)
            if done:
                for q in qs:
                    acc[q] = acc[q] + jnp.where((lane >= spoiled) & (lane < LANES - spoiled), inner[q], 0.0)

    for k in range(tiles):
        node_ref[pl.ds(k, LANES, stride=tiles), :] = jnp.transpose(x_ref[:, cols(k)])
    side = lax.broadcasted_iota(jnp.int32, (block, LANES), 1)
    strip = e_ref[(steps - 1) % 2, 0]
    for t in range(tiles):
        z = jnp.transpose(node_ref[cols(t), :])
        if t == 0:
            z = jnp.where(side < steps, strip, z)
        if t == tiles - 1:
            z = jnp.where(side >= LANES - steps, strip, z)
        out_ref[:, cols(t)] = z
    if last:
        total = sum_ref[...]
        for q in range(groups):
            both = acc[q] + before_ref[rows(q), :]
            out_ref[rows(q), cols(tiles)] = both + pltpu.roll(both, HALF, 1)
            total = total + both
        sum_ref[...] = total
    else:
        for q in range(groups):
            sum_ref[rows(q), :] = acc[q]


def finish_kernel(sources, steps, share, a_ref, b_ref, a0_ref, b0_ref, p_ref, out_ref, price_ref, total_ref):
    width = a_ref.shape[2]
    per = a_ref.shape[0]
    i = pl.program_id(0)
    lane = lax.broadcasted_iota(jnp.int32, (ROWS, LANES), 1)
    for j in range(per):
        left = lax.rem(i * per + j + sources - 1, sources)
        for h, ref in enumerate((a_ref, b_ref)):
            at = (2 * j + h) * width
            head = b0_ref[left] if h == 0 else a0_ref[i * per + j]
            out_ref[:, at : at + LANES] = jnp.where(lane < steps, head, ref[j, :, 0:LANES])
            out_ref[:, at + LANES : at + width] = ref[j, :, LANES:width]

    @pl.when(i == 0)
    def _():
        both = p_ref[0]
        for j in range(1, sources):
            both = both + p_ref[j]
        total_ref[0] = jnp.sum(jnp.where(lane >= HALF, both, 0.0)) / share
        mine = jnp.where(lane < HALF, both, 0.0)
        for r in range(ROWS):
            price_ref[r] = jnp.sum(mine[r : r + 1, :])


def whole(shape, index=None):
    at = index if index is not None else (0,) * len(shape)
    return pl.BlockSpec(shape, lambda i: at)


def vmem(*shape):
    return pltpu.VMEM(shape, jnp.float32)


def roll_chunk(h, far, values_in, table, price_rows, beyond, beyond_specs, trades, before):
    n, total_width = values_in.shape
    steps = table[0].shape[0]
    width = total_width // CHUNKS
    tiles = width // LANES
    block = LANES
    last = h == CHUNKS - 1
    out_width = width + LANES if last else width
    f32 = jnp.float32
    row_block = pl.BlockSpec((block, LANES), lambda i: (i, 0))
    return pl.pallas_call(
        functools.partial(roll_kernel, last),
        grid=(n // block,),
        in_specs=[pl.BlockSpec(memory_space=pltpu.SMEM), pl.BlockSpec((block, width), lambda i: (i, h))]
        + [whole((steps, width), (0, h))] * 5
        + [whole((tiles, LANES), (h, 0))]
        + beyond_specs
        + [whole(z.shape) for z in trades]
        + ([row_block] if last else []),
        out_specs=[
            pl.BlockSpec((block, out_width), lambda i: (i, 0)),
            whole((ROWS, LANES)) if last else row_block,
        ],
        out_shape=[
            jax.ShapeDtypeStruct((n, out_width), f32),
            jax.ShapeDtypeStruct((ROWS, LANES) if last else (n, LANES), f32),
        ],
        scratch_shapes=[
            vmem(LANES, width),
            vmem(LANES, width),
            vmem(LANES, LANES),
            vmem(block, width),
            vmem(width, LANES),
            vmem(2, block, width),
            vmem(2, 2, block, LANES),
            vmem(2, 3, block, LANES),
            vmem(n, LANES),
            vmem(n, LANES),
            pltpu.VMEM((n, LANES), jnp.int32),
        ],
        cost_estimate=pl.CostEstimate(
            flops=12 * n * width * steps, bytes_accessed=3 * 4 * n * width, transcendentals=0
        ),
        name="roll_last" if last else "roll_first",
    )(far, values_in, *table, price_rows, *beyond, *trades, *before)


def local(values_in, prob_up, prob_down, discount, swap_rate, annuity, state_price, exercise_step, strike_bucket, notional_sign, strike_table):
    n, total_width = values_in.shape
    steps = prob_up.shape[0]
    node_count = lax.axis_size(NODE)
    trade_count = lax.axis_size("trade")
    width = total_width // CHUNKS
    tiles = width // LANES
    table = (prob_up, prob_down, discount, swap_rate, annuity)
    price_rows = state_price.reshape(-1, LANES)
    trades = (exercise_step.T, strike_bucket.reshape(-1, LANES), notional_sign.reshape(-1, LANES), strike_table.reshape(1, -1))
    f32 = jnp.float32
    block = LANES

    halo_rows = n + 5 * steps + ROWS
    packed = pl.pallas_call(
        pack_kernel,
        grid=(1,),
        in_specs=[whole((n, LANES))] + [whole((steps, LANES))] * 5 + [whole(price_rows.shape)],
        out_specs=whole((halo_rows, LANES)),
        out_shape=jax.ShapeDtypeStruct((halo_rows, LANES), f32),
        name="pack",
    )(values_in, *table, price_rows)
    halo = lax.ppermute(packed, NODE, [((i + 1) % node_count, i) for i in range(node_count)])
    far = (lax.axis_index(NODE) == node_count - 1).astype(jnp.int32).reshape(1)

    inner_specs = (
        [pl.BlockSpec((block, LANES), lambda i: (i, tiles))]
        + [whole((steps, LANES), (0, tiles))] * 5
        + [whole((tiles, LANES), (1, 0))]
    )
    first, first_sums = roll_chunk(
        0, jnp.zeros((1,), jnp.int32), values_in, table, price_rows,
        (values_in,) + table + (price_rows,), inner_specs, trades, (),
    )
    halo_specs = (
        [pl.BlockSpec((block, LANES), lambda i: (i, 0))]
        + [whole((steps, LANES), (n // steps + j, 0)) for j in range(5)]
        + [whole((ROWS, LANES), ((n + 5 * steps) // ROWS, 0))]
    )
    rows = n // node_count
    first_moved = lax.all_to_all(first.reshape(node_count, rows, width), NODE, 0, 0, tiled=True)
    second, sums = roll_chunk(
        1, far, values_in, table, price_rows, (halo,) * 7, halo_specs, trades, (first_sums,)
    )
    total = sums
    for k in range(1, trade_count):
        total = total + lax.ppermute(sums, "trade", [(i, (i + k) % trade_count) for i in range(trade_count)])
    total = total + jnp.roll(total, HALF, axis=1)
    lane = lax.broadcasted_iota(jnp.int32, (node_count, rows, LANES), 2)
    blocks = second.reshape(node_count, rows, width + LANES)
    tail = jnp.where(lane < HALF, blocks[:, :, width:], total[None])
    blocks = lax.dynamic_update_slice_in_dim(blocks, tail, width, 2)
    second_moved = lax.all_to_all(blocks, NODE, 0, 0, tiled=True)

    per = 4
    values, prices, portfolio = pl.pallas_call(
        functools.partial(finish_kernel, node_count, steps, float(n)),
        grid=(node_count // per,),
        in_specs=[
            pl.BlockSpec((per, rows, width), lambda i: (i, 0, 0)),
            pl.BlockSpec((per, rows, width), lambda i: (i, 0, 0)),
            whole((node_count, rows, LANES)),
            whole((node_count, rows, LANES)),
            whole((node_count, rows, LANES), (0, 0, tiles)),
        ],
        out_specs=[
            pl.BlockSpec((rows, per * total_width), lambda i: (0, i)),
            pl.BlockSpec(memory_space=pltpu.SMEM),
            pl.BlockSpec(memory_space=pltpu.SMEM),
        ],
        out_shape=[
            jax.ShapeDtypeStruct((rows, node_count * total_width), f32),
            jax.ShapeDtypeStruct((rows,), f32),
            jax.ShapeDtypeStruct((1,), f32),
        ],
        name="finish",
    )(first_moved, second_moved, first_moved, second_moved, second_moved)
    return values, prices, portfolio.reshape(())


def solution(mesh):
    split = Mesh(mesh.devices.reshape(mesh.shape["trade"], 4, 4, 2), TRADE_NODE)
    in_specs = (
        P("trade", NODE),
        P(None, NODE),
        P(None, NODE),
        P(None, NODE),
        P(None, NODE),
        P(None, NODE),
        P(NODE),
        P("trade", None),
        P("trade"),
        P("trade"),
        P(),
    )
    out_specs = (P(TRADE_NODE, None), P(TRADE_NODE), P())
    return jax.shard_map(local, mesh=split, in_specs=in_specs, out_specs=out_specs, check_vma=False)
```

time: 93.9 us -> 77.8 us (0.83)
  the two profiles are of different devices: /device:TPU:6 before, /device:TPU:1 now
where the time goes in v2:
time: 77.8 us; the launch traced here: 77.2 us
  blocking collectives  27.9 us (36%)
  Pallas kernels  27.8 us (36%)
  starting transfers between devices  14.3 us (18%)
  waiting for transfers between devices  3.47 us (4%)
  other arithmetic  2.34 us (3%)
    all_to_all x1, blocking collectives, local(): second_moved = lax.all_to_all(blocks, NODE, 0, 0, tiled=True)  27.9 us
    pallas_call x2, Pallas kernels, roll_chunk(): pl.pallas_call(functools.partial(roll_kernel, last), grid=(n // block,),...  20.1 us
    all_to_all x1, starting transfers between devices, local(): lax.all_to_all(first.reshape(node_count, rows, width), NODE, 0, 0, tiled=...  8.35 us
    pallas_call x1, Pallas kernels, local(): pl.pallas_call(functools.partial(finish_kernel, node_count, steps, float(...  6.11 us
    ppermute x3, starting transfers between devices, local(): lax.ppermute(sums, 'trade', [(i, (i + k) % trade_count) for i in range(tr...  4.52 us
    ppermute x3, waiting for transfers between devices, local(): lax.ppermute(sums, 'trade', [(i, (i + k) % trade_count) for i in range(tr...  3.47 us
    pallas_call x1, Pallas kernels, local(): pl.pallas_call(pack_kernel, grid=(1,), in_specs=[whole((n, LANES))] + [wh...  1.65 us
    dynamic_update_slice x1, other arithmetic, local(): blocks = lax.dynamic_update_slice_in_dim(blocks, tail, width, 2)  1.57 us
  transfers between devices with their start and end apart: 5, of which 2 were waited for; matrix products, arithmetic and copies ran while one was open for 3% of the time, Pallas kernels for 26%

profile of v2, /device:TPU:1, one launch (start us, length us, event | category | flops | bytes accessed | tf_op | source)
XLA Modules:
  0.0 77.2 jit_solution(882617286619800451)
XLA Ops:
  0.6 1.6 %pack.1 = f32[344,128]{1,0:T(8,128)} custom-call(f32[256,2048]{1,0:T(8,128)} %v_ref.5, f32[16,2048]{1,0:T(8,128)} %up_ref.5, f32[16,2048]{1,0:T(8,128)} %dn_ref.5, f32[16,2048]{1,0:T(8,128)} %dc_ref.5, f32[16,2048]{1,0:T(8,128)} %sr_ref.5, f32[16,2048]{1,0:T(8,128)} %an_ref.5, f32[16,128]{1,0:T(8,128)} %bitcast.11), custom_call_target="tpu_custom_call" | custom-call | tf_op jit(solution)/shard_map/pack/pallas_call | solution.py:318
  2.3 1.4 %collective-permute-start = (f32[344,128]{1,0:T(8,128)}, f32[344,128]{1,0:T(8,128)S(1)}, u32[]{:S(2)}, u32[]{:S(2)}) collective-permute-start(f32[344,128]{1,0:T(8,128)} %pack.1), channel_id=1, source_target_pairs={{1,0},{2,1},{3,2},{4,3},{5,4},{6,5},{7,6},{8,7},{9,8},{10,9},{11,1... | collective-permute-start | bytes 528392 | tf_op jit(solution)/shard_map/ppermute | solution.py:326
  3.7 10.0 %roll_first.1 = (f32[256,1024]{1,0:T(8,128)}, f32[256,128]{1,0:T(8,128)}) custom-call(s32[1]{0:T(128)} %constant.9.clone.1.far_ref, f32[256,2048]{1,0:T(8,128)} %v_ref.5, f32[16,2048]{1,0:T(8,128)} %up_ref.5, f32[16,2048]{1,0:T(8,128)} %dn_ref.5, f32[16,2048]{1,0:T(8,128)} %dc_ref.5, f32[16,2048]{1,0:T(8,128)} %sr_ref.5, f32[16,2048]{1,0:T(8,128)} %an_ref.5, ...), custom_call_target="tpu_custom_call" | custom-call | flops 50331648 | bytes 3145728 | tf_op jit(solution)/shard_map/roll_first/pallas_call | solution.py:267
  13.6 8.4 %all-to-all-start = ((f32[32,8,1024]{2,1,0:T(8,128)}), f32[32,8,1024]{2,1,0:T(8,128)S(1)}, u32[]{:S(2)}, u32[]{:S(2)}) async-start(f32[32,8,1024]{2,1,0:T(8,128)} %bitcast.10), calls=%async_computation | async-start | bytes 2097152 | tf_op jit(solution)/shard_map/all_to_all | solution.py:344
  22.0 0.0 collective-permute-done.v2_ref.up2_ref.dn2_ref.dc2_ref.sr2_ref.an2_ref.sp2_ref
  22.0 0.0 copy-start.1
  22.0 0.7 copy-done.1
  22.7 10.1 %roll_last.1 = (f32[256,1152]{1,0:T(8,128)}, f32[8,128]{1,0:T(8,128)}) custom-call(s32[1]{0:T(128)} %bitcast.6.far_ref, f32[256,2048]{1,0:T(8,128)} %v_ref.5, f32[16,2048]{1,0:T(8,128)} %up_ref.5, f32[16,2048]{1,0:T(8,128)} %dn_ref.5, f32[16,2048]{1,0:T(8,128)} %dc_ref.5, f32[16,2048]{1,0:T(8,128)} %sr_ref.5, f32[16,2048]{1,0:T(8,128)} %an_ref.5, ...), custom_call_target="tpu_custom_call" | custom-call | flops 50331648 | bytes 3145728 | tf_op jit(solution)/shard_map/roll_last/pallas_call | solution.py:267
  32.8 3.8 %collective-permute-start.3 = (f32[8,128]{1,0:T(8,128)}, f32[8,128]{1,0:T(8,128)S(1)}, u32[]{:S(2)}, u32[]{:S(2)}) collective-permute-start(f32[8,128]{1,0:T(8,128)} %get-tuple-element.13), channel_id=1, source_target_pairs={{0,96},{32,0},{64,32},{96,64},{1,97},{33,1},{65,33},{97,65},{2,98}... | collective-permute-start | bytes 12296 | tf_op jit(solution)/shard_map/ppermute | solution.py:350
  36.6 0.0 collective-permute-start.2
  36.6 0.7 collective-permute-start.1
  37.3 0.3 collective-permute-done.3
  37.6 3.2 %collective-permute-done.2 = f32[8,128]{1,0:T(8,128)S(1)} collective-permute-done((f32[8,128]{1,0:T(8,128)}, f32[8,128]{1,0:T(8,128)S(1)}, u32[]{:S(2)}, u32[]{:S(2)}) %collective-permute-start.2) | collective-permute-done | bytes 4128 | tf_op jit(solution)/shard_map/ppermute | solution.py:350
  40.8 0.0 collective-permute-done.1
  40.8 0.7 add_add_fusion
  41.5 0.1 fusion.1
  41.5 0.1 maximum_add_fusion
  41.6 1.6 %fusion = f32[32,8,1152]{2,1,0:T(8,128)} fusion(f32[32,8,1152]{2,1,0:T(8,128)} %bitcast.9, f32[8,128]{1,0:T(8,128)S(1)} %maximum_add_fusion, pred[128]{0:T(512)(128)(4,1)S(1)} %iota_compare_fusion), kind=kLoop, calls=%fused_computation.1 | loop fusion | flops 32768 | bytes 266368 | tf_op jit(solution)/shard_map/dynamic_update_slice | solution.py:355
  43.2 0.0 all-to-all-done.a_ref.a0_ref
  43.2 0.0 copy-start
  43.2 27.9 %all_to_all.10.b_ref.b0_ref.p_ref = f32[32,8,1152]{2,1,0:T(8,128)} all-to-all(f32[32,8,1152]{2,1,0:T(8,128)} %fusion), channel_id=1, replica_groups=mesh['trade'=4,'node_0'=4,'node_1'=4,'node_2'=2] {'node_0','node_1','nod..., dimensions={0} | all-to-all | bytes 2359296 | tf_op jit(solution)/shard_map/all_to_all | solution.py:356
  71.1 0.0 copy-done
  71.1 6.1 %finish.1 = (f32[8,65536]{1,0:T(8,128)}, f32[8]{0:T(128)}, f32[1]{0:T(128)}) custom-call(f32[32,8,1024]{2,1,0:T(8,128)} %copy-done, f32[32,8,1152]{2,1,0:T(8,128)} %all_to_all.10.b_ref.b0_ref.p_ref, f32[32,8,1024]{2,1,0:T(8,128)} %copy-done, f32[32,8,1152]{2,1,0:T(8,128)} %all_to_all.10.b_ref.b0_ref.p_ref, f32[32,8,1152]{2,1,0:T(8,128)} %all_to_all.10.b_ref.b0_ref.p_ref), custom_call_target="tpu_custom_call" | custom-call | tf_op jit(solution)/shard_map/finish/pallas_call | solution.py:359
  (1 shorter events, 0.0 us)
Async XLA Ops:
  2.3 19.7 %collective-permute-start = (f32[344,128]{1,0:T(8,128)}, f32[344,128]{1,0:T(8,128)S(1)}, u32[]{:S(2)}, u32[]{:S(2)}) collective-permute-start(f32[344,128]{1,0:T(8,128)} %pack.1), channel_id=1, source_target_pairs={{1,0},{2,1},{3,2},{4,3},{5,4},{6,5},{7,6},{8,7},{9,8},{10,9},{11,1... | collective-permute-start | bytes 528392 | tf_op jit(solution)/shard_map/ppermute | solution.py:326
  13.6 29.6 %all-to-all-start = ((f32[32,8,1024]{2,1,0:T(8,128)}), f32[32,8,1024]{2,1,0:T(8,128)S(1)}, u32[]{:S(2)}, u32[]{:S(2)}) async-start(f32[32,8,1024]{2,1,0:T(8,128)} %bitcast.10), calls=%async_computation | async-start | bytes 2097152 | tf_op jit(solution)/shard_map/all_to_all | solution.py:344
  22.0 0.7 copy-start.1
  32.8 4.8 %collective-permute-start.3 = (f32[8,128]{1,0:T(8,128)}, f32[8,128]{1,0:T(8,128)S(1)}, u32[]{:S(2)}, u32[]{:S(2)}) collective-permute-start(f32[8,128]{1,0:T(8,128)} %get-tuple-element.13), channel_id=1, source_target_pairs={{0,96},{32,0},{64,32},{96,64},{1,97},{33,1},{65,33},{97,65},{2,98}... | collective-permute-start | bytes 12296 | tf_op jit(solution)/shard_map/ppermute | solution.py:350
  36.6 4.2 %collective-permute-start.2 = (f32[8,128]{1,0:T(8,128)}, f32[8,128]{1,0:T(8,128)S(1)}, u32[]{:S(2)}, u32[]{:S(2)}) collective-permute-start(f32[8,128]{1,0:T(8,128)} %get-tuple-element.13), channel_id=1, source_target_pairs={{0,64},{32,96},{64,0},{96,32},{1,65},{33,97},{65,1},{97,33},{2,66}... | collective-permute-start | bytes 12296 | tf_op jit(solution)/shard_map/ppermute | solution.py:350
  36.6 4.2 %collective-permute-start.1 = (f32[8,128]{1,0:T(8,128)}, f32[8,128]{1,0:T(8,128)S(1)}, u32[]{:S(2)}, u32[]{:S(2)}) collective-permute-start(f32[8,128]{1,0:T(8,128)} %get-tuple-element.13), channel_id=1, source_target_pairs={{0,32},{32,64},{64,96},{96,0},{1,33},{33,65},{65,97},{97,1},{2,34}... | collective-permute-start | bytes 12296 | tf_op jit(solution)/shard_map/ppermute | solution.py:350
  43.2 27.9 %copy-start = (f32[32,8,1024]{2,1,0:T(8,128)}, f32[32,8,1024]{2,1,0:T(8,128)S(1)}, u32[]{:S(2)}) copy-start(f32[32,8,1024]{2,1,0:T(8,128)S(1)} %all-to-all-done.a_ref.a0_ref) | copy-start | bytes 3145732

commit v3 on v0

v3 whole, which is shorter than its diff:
```python
import functools

import jax
import jax.numpy as jnp
from jax import lax
from jax.experimental import pallas as pl
from jax.experimental.pallas import tpu as pltpu
from jax.sharding import Mesh
from jax.sharding import PartitionSpec as P

LANES = 128
HALF = LANES // 2
ROWS = 8
FIRST_TILES = 10
TOGETHER = 4
OFF = 1e30
NODE = ("node_0", "node_1", "node_2")
TRADE_NODE = ("trade",) + NODE


def scaled_rows(up, down, disc, ann):
    row = lax.broadcasted_iota(jnp.int32, ann.shape, 0)
    width = ann.shape[1]
    before = jnp.where(row == 0, 1.0, pltpu.roll(ann, 1, 0))
    share = disc / ann
    a = share * up * pltpu.roll(before, width - 1, 1)
    b = share * (1.0 - up - down) * before
    c = share * down * pltpu.roll(before, 1, 1)
    return a, b, c


def trade_columns(ex_ref, bucket_ref, sign_ref, table_ref, half):
    ex = ex_ref[:, half * LANES : (half + 1) * LANES]
    bits = jnp.left_shift(jnp.ones_like(ex), ex)
    mask = bits[0:1] | bits[1:2] | bits[2:3] | bits[3:4]
    bucket = bucket_ref[half : half + 1, :]
    levels = lax.broadcasted_iota(jnp.int32, (table_ref.shape[1], LANES), 0)
    strike = jnp.dot(
        table_ref[...],
        (levels == bucket).astype(jnp.float32),
        precision=lax.Precision.HIGHEST,
        preferred_element_type=jnp.float32,
    )
    sign = (2 * sign_ref[half : half + 1, :] - 1).astype(jnp.float32)

    def column(r):
        return jnp.transpose(jnp.broadcast_to(r, (LANES, LANES)))

    return column(sign), column(sign * strike), column(mask.astype(jnp.float32)).astype(jnp.int32)


def on_terms(sign, key, mask, step):
    on = (mask & (1 << step)) != 0
    return jnp.where(on, sign, 0.0), jnp.where(on, key, OFF)


def roll_kernel(start, last, far_ref, v_ref, up_ref, dn_ref, dc_ref, sr_ref, an_ref, *rest):
    smalls, rest = rest[:5], rest[5:]
    if last:
        halo_ref, before_ref, out_ref, price_ref, sum_ref = rest[:5]
    else:
        out_ref, sum_ref, pack_ref, pack_sems = rest[0], rest[1], rest[2], rest[-1]
        rest = rest[:-1]
    (
        nat_ref, coef_ref, strip_ref, x_ref, node_ref, buf_ref, rim_ref, e_ref, sgn_ref, key_ref, mask_ref,
        own_ref, table_ref, stage_ref, table_sems, own_sems, out_sems,
        sp_ref, ex_ref, bk_ref, sg_ref, tb_ref, small_sems,
    ) = rest[-23:]
    n, steps = v_ref.shape[0], up_ref.shape[0]
    width = x_ref.shape[1]
    stop = start + width
    tiles = width // LANES
    block = x_ref.shape[0]
    groups = block // ROWS
    lane = lax.broadcasted_iota(jnp.int32, (ROWS, LANES), 1)

    def cols(k):
        return slice(k * LANES, (k + 1) * LANES)

    def rows(q):
        return slice(q * ROWS, (q + 1) * ROWS)

    def spread(src, dst):
        for t in range(tiles):
            node_ref[cols(t), :] = jnp.transpose(src(t))
        for k in range(tiles):
            dst[:, cols(k)] = jnp.transpose(node_ref[pl.ds(k, LANES, stride=tiles), :])

    seen = own_ref.shape[1]
    from_start = pl.ds(start, seen)
    table_copies = [
        pltpu.make_async_copy(ref.at[:, from_start], table_ref.at[j], table_sems.at[j])
        for j, ref in enumerate((up_ref, dn_ref, dc_ref, sr_ref, an_ref))
    ]
    own_copies = [
        pltpu.make_async_copy(
            v_ref.at[pl.ds(i * block, block), from_start], own_ref.at[pl.ds(i * block, block), :], own_sems.at[i]
        )
        for i in range(n // block)
    ]
    small_copies = [
        pltpu.make_async_copy(src, dst, small_sems.at[j])
        for j, (src, dst) in enumerate(zip(smalls, (sp_ref, ex_ref, bk_ref, sg_ref, tb_ref)))
    ]
    for copy in small_copies + table_copies + own_copies:
        copy.start()
    for copy in small_copies:
        copy.wait()
    for half in range(n // LANES):
        sign, key, mask = trade_columns(ex_ref, bk_ref, sg_ref, tb_ref, half)
        at = pl.ds(half * LANES, LANES)
        sgn_ref[at, :] = sign
        key_ref[at, :] = key
        mask_ref[at, :] = mask
    if last:
        sum_ref[...] = jnp.zeros((ROWS, LANES), jnp.float32)
    for copy in table_copies:
        copy.wait()
    pack_copies = []
    if not last:
        tile = pl.ds(0, LANES)
        pack_copies = [
            pltpu.make_async_copy(table_ref.at[j, :, tile], pack_ref.at[pl.ds(n + j * steps, steps), :], pack_sems.at[j])
            for j in range(5)
        ]
        pack_copies.append(
            pltpu.make_async_copy(
                sp_ref.at[pl.ds(0, ROWS), :], pack_ref.at[pl.ds(n + 5 * steps, ROWS), :], pack_sems.at[5]
            )
        )
        for copy in pack_copies:
            copy.start()

    up, dn, dc, sr, an = (table_ref[j, :, 0:width] for j in range(5))
    a, b, c = scaled_rows(up, dn, dc, an)
    for j, z in enumerate((a, b, c, sr)):
        nat_ref[j * steps : (j + 1) * steps, :] = z
    nat_ref[4 * steps : 4 * steps + ROWS, :] = an[steps - ROWS : steps, :]
    for t in range(tiles):
        price = sp_ref[start // LANES + t : start // LANES + t + 1, :]
        if t == 0:
            price = jnp.where(lane < steps, 0.0, price)
        if t == tiles - 1:
            price = jnp.where(lane >= LANES - steps, 0.0, price)
        nat_ref[4 * steps + ROWS : 4 * steps + 2 * ROWS, cols(t)] = jnp.broadcast_to(price, (ROWS, LANES))
    nat_ref[4 * steps + 2 * ROWS :, :] = jnp.zeros((LANES - 4 * steps - 2 * ROWS, width), jnp.float32)
    spread(lambda t: nat_ref[:, cols(t)], coef_ref)

    side = lax.broadcasted_iota(jnp.int32, (steps, LANES), 1)

    def joined(j):
        beyond = halo_ref[n + j * steps : n + (j + 1) * steps, :] if last else table_ref[j, :, width:seen]
        return jnp.where(side < HALF, beyond, table_ref[j, :, width - LANES : width])

    strip_an = joined(4)
    a, b, c = scaled_rows(joined(0), joined(1), joined(2), strip_an)
    if last:
        far = far_ref[0] == 1
        a = jnp.where((side == LANES - 1) & far, 0.0, a)
        c = jnp.where((side == 0) & far, 0.0, c)
    for j, z in enumerate((a, b, c, joined(3))):
        strip_ref[j * steps : (j + 1) * steps, :] = z
    strip_ref[4 * steps : 4 * steps + ROWS, :] = strip_an[steps - ROWS : steps, :]
    beyond = halo_ref[n + 5 * steps : n + 5 * steps + 1, :] if last else sp_ref[stop // LANES : stop // LANES + 1, :]
    price = jnp.where(lane < HALF, beyond, sp_ref[stop // LANES - 1 : stop // LANES, :])
    strip_ref[4 * steps + ROWS : 4 * steps + 2 * ROWS, :] = jnp.where(
        (lane < steps) | (lane >= LANES - steps), price, 0.0
    )

    def wide(ref, r, at):
        return jnp.broadcast_to(ref[r : r + 1, at], (ROWS, LANES))

    def load(s, q, k):
        return x_ref[rows(q), cols(k)] if s == 0 else buf_ref[(s - 1) % 2, rows(q), cols(k)]

    def put_rim(s, q, first, final):
        rim_ref[s % 2, 0, rows(q), :] = pltpu.roll(first, LANES - 1, 1)
        rim_ref[s % 2, 1, rows(q), :] = pltpu.roll(final, 1, 1)

    def put_strip(s, q, e):
        e_ref[s % 2, 0, rows(q), :] = e
        e_ref[s % 2, 1, rows(q), :] = pltpu.roll(e, LANES - 1, 1)
        e_ref[s % 2, 2, rows(q), :] = pltpu.roll(e, 1, 1)

    @pl.loop(0, n // block)
    def _(i):
        all_rows = pl.ds(pl.multiple_of(i * block, block), block)
        base = [pl.ds(pl.multiple_of(i * block + ROWS * q, ROWS), ROWS) for q in range(groups)]
        pltpu.make_async_copy(
            v_ref.at[all_rows, from_start], own_ref.at[all_rows, :], own_sems.at[i]
        ).wait()
        if not last:
            pltpu.make_async_copy(
                own_ref.at[all_rows, pl.ds(0, LANES)], pack_ref.at[all_rows, :], pack_sems.at[6 + i]
            ).start()
        spread(lambda t: own_ref[all_rows, cols(t)], x_ref)
        for q in range(groups):
            put_rim(1, q, load(0, q, 0), load(0, q, tiles - 1))
            beyond = halo_ref[base[q], :] if last else own_ref[base[q], width:seen]
            put_strip(1, q, jnp.where(lane < HALF, beyond, own_ref[base[q], width - LANES : width]))
        acc = [None] * groups
        for s in range(steps):
            done = s == steps - 1
            for q0 in range(0, groups, TOGETHER):
                qs = range(q0, q0 + TOGETHER)
                terms = {q: on_terms(sgn_ref[base[q], :], key_ref[base[q], :], mask_ref[base[q], :], s) for q in qs}
                a, b, c, p = (wide(strip_ref, j * steps + s, slice(None)) for j in range(4))
                for q in qs:
                    alpha, beta = terms[q]
                    z = (s + 1) % 2
                    e = a * e_ref[z, 1, rows(q), :] + b * e_ref[z, 0, rows(q), :] + c * e_ref[z, 2, rows(q), :]
                    e = jnp.maximum(e, alpha * p - beta)
                    if done:
                        e = e * strip_ref[4 * steps + ROWS - 1 : 4 * steps + ROWS, :]
                        e_ref[s % 2, 0, rows(q), :] = e
                        acc[q] = e * strip_ref[4 * steps + ROWS : 4 * steps + 2 * ROWS, :]
                    else:
                        put_strip(s, q, e)
                below = {q: rim_ref[(s + 1) % 2, 1, rows(q), :] for q in qs}
                here = {q: load(s, q, 0) for q in qs}
                first = {}
                for k in range(tiles):
                    a, b, c, p = (wide(coef_ref, j * steps + s, cols(k)) for j in range(4))
                    if done:
                        fin = wide(coef_ref, 4 * steps + ROWS - 1, cols(k))
                        price = wide(coef_ref, 4 * steps + ROWS, cols(k))
                    for q in qs:
                        above = load(s, q, k + 1) if k + 1 < tiles else rim_ref[(s + 1) % 2, 0, rows(q), :]
                        alpha, beta = terms[q]
                        new = jnp.maximum(a * above + b * here[q] + c * below[q], alpha * p - beta)
                        below[q], here[q] = here[q], above
                        if done:
                            new = new * fin
                            x_ref[rows(q), cols(k)] = new
                            acc[q] = acc[q] + new * price
                        else:
                            buf_ref[s % 2, rows(q), cols(k)] = new
                            if k == 0:
                                first[q] = new
                            if k == tiles - 1:
                                put_rim(s, q, first[q], new)

        for k in range(tiles):
            node_ref[pl.ds(k, LANES, stride=tiles), :] = jnp.transpose(x_ref[:, cols(k)])
        rim = lax.broadcasted_iota(jnp.int32, (block, LANES), 1)
        strip = e_ref[(steps - 1) % 2, 0]
        for t in range(tiles):
            z = jnp.transpose(node_ref[cols(t), :])
            if t == 0:
                z = jnp.where(rim < steps, strip, z)
            if t == tiles - 1:
                z = jnp.where(rim >= LANES - steps, strip, z)
            stage_ref[all_rows, cols(t)] = z
            here = pl.ds(t * LANES, LANES)
            pltpu.make_async_copy(stage_ref.at[all_rows, here], out_ref.at[all_rows, here], out_sems.at[i, t]).start()
        if last:
            total = sum_ref[...]
            for q in range(groups):
                both = acc[q] + before_ref[base[q], :]
                price_ref[base[q], :] = both + pltpu.roll(both, HALF, 1)
                total = total + both
            sum_ref[...] = total
        else:
            for q in range(groups):
                sum_ref[base[q], :] = acc[q]

    for i in range(n // block):
        at = pl.ds(i * block, block)
        for t in range(tiles):
            tile = pl.ds(t * LANES, LANES)
            pltpu.make_async_copy(stage_ref.at[at, tile], out_ref.at[at, tile], out_sems.at[i, t]).wait()
        if not last:
            pltpu.make_async_copy(
                own_ref.at[at, pl.ds(0, LANES)], pack_ref.at[at, :], pack_sems.at[6 + i]
            ).wait()
    for copy in pack_copies:
        copy.wait()


def tail_kernel(sum_ref, *refs):
    *moved, price_ref, old_ref, out_ref, tail_ref, sem = refs
    del old_ref
    total = sum_ref[...]
    for ref in moved:
        total = total + ref[...]
    total = total + pltpu.roll(total, HALF, 1)
    lane = lax.broadcasted_iota(jnp.int32, (ROWS, LANES), 1)
    for q in range(tail_ref.shape[0] // ROWS):
        rows = slice(q * ROWS, (q + 1) * ROWS)
        tail_ref[rows, :] = jnp.where(lane < HALF, price_ref[rows, :], total)
    copy = pltpu.make_async_copy(tail_ref, out_ref.at[:, pl.ds(out_ref.shape[1] - LANES, LANES)], sem)
    copy.start()
    copy.wait()


def first_half_kernel(sources, total_width, a_ref, out_ref, sems):
    width = a_ref.shape[2]
    copies = [
        pltpu.make_async_copy(
            a_ref.at[j, :, pl.ds(LANES, width - LANES)],
            out_ref.at[:, pl.ds(j * total_width + LANES, width - LANES)],
            sems.at[j],
        )
        for j in range(sources)
    ]
    for copy in copies:
        copy.start()
    for copy in copies:
        copy.wait()


def second_half_kernel(
    sources, total_width, steps, share, a_ref, b_ref, old_ref, out_ref, price_ref, total_ref, head_ref, body_ref, sems
):
    del old_ref
    width = total_width - a_ref.shape[2]
    lane = lax.broadcasted_iota(jnp.int32, (ROWS, LANES), 1)
    copies = []
    for j in range(sources):
        left = (j + sources - 1) % sources
        at = slice(j * width, j * width + LANES)
        head_ref[:, j * LANES : (j + 1) * LANES] = jnp.where(
            lane < steps, b_ref[left, :, 0:LANES], a_ref[j, :, 0:LANES]
        )
        body_ref[:, at] = jnp.where(lane < steps, a_ref[j, :, 0:LANES], b_ref[j, :, 0:LANES])
        body_ref[:, j * width + LANES : (j + 1) * width] = b_ref[j, :, LANES:width]
        copies.append(
            pltpu.make_async_copy(
                head_ref.at[:, pl.ds(j * LANES, LANES)],
                out_ref.at[:, pl.ds(j * total_width, LANES)],
                sems.at[0, j],
            )
        )
        copies.append(
            pltpu.make_async_copy(
                body_ref.at[:, pl.ds(j * width, width)],
                out_ref.at[:, pl.ds((j + 1) * total_width - width, width)],
                sems.at[1, j],
            )
        )
        copies[-2].start()
        copies[-1].start()
    both = b_ref[0, :, width:]
    for j in range(1, sources):
        both = both + b_ref[j, :, width:]
    total_ref[0] = jnp.sum(jnp.where(lane >= HALF, both, 0.0)) / share
    mine = jnp.where(lane < HALF, both, 0.0)
    for r in range(ROWS):
        price_ref[r] = jnp.sum(mine[r : r + 1, :])
    for copy in copies:
        copy.wait()


def vmem(*shape):
    return pltpu.VMEM(shape, jnp.float32)


HERE = pl.BlockSpec(memory_space=pltpu.VMEM)
SCALARS = pl.BlockSpec(memory_space=pltpu.SMEM)
FAR = pl.BlockSpec(memory_space=pltpu.HBM)


def here(x):
    return pltpu.with_memory_space_constraint(x, pltpu.VMEM)


def roll_chunk(start, width, far, arrays, extra):
    n, total_width = arrays[0].shape
    steps = arrays[1].shape[0]
    last = start + width == total_width
    out_width = width + LANES if last else width
    seen = width if last else width + LANES
    f32 = jnp.float32
    return pl.pallas_call(
        functools.partial(roll_kernel, start, last),
        in_specs=[SCALARS] + [FAR] * len(arrays) + [HERE] * len(extra),
        out_specs=[FAR, HERE, HERE if last else FAR],
        out_shape=[
            jax.ShapeDtypeStruct((n, out_width), f32),
            jax.ShapeDtypeStruct((n, LANES), f32),
            jax.ShapeDtypeStruct((ROWS if last else n + 5 * steps + ROWS, LANES), f32),
        ],
        scratch_shapes=[
            vmem(LANES, width),
            vmem(LANES, width),
            vmem(LANES, LANES),
            vmem(LANES, width),
            vmem(width, LANES),
            vmem(2, LANES, width),
            vmem(2, 2, LANES, LANES),
            vmem(2, 3, LANES, LANES),
            vmem(n, LANES),
            vmem(n, LANES),
            pltpu.VMEM((n, LANES), jnp.int32),
            vmem(n, seen),
            vmem(5, steps, seen),
            vmem(n, width),
            pltpu.SemaphoreType.DMA((5,)),
            pltpu.SemaphoreType.DMA((n // LANES,)),
            pltpu.SemaphoreType.DMA((n // LANES, width // LANES)),
        ]
        + [pltpu.VMEM(z.shape, z.dtype) for z in arrays[6:]]
        + [pltpu.SemaphoreType.DMA((5,))]
        + ([] if last else [pltpu.SemaphoreType.DMA((6 + n // LANES,))]),
        cost_estimate=pl.CostEstimate(
            flops=12 * n * width * steps, bytes_accessed=3 * 4 * n * width, transcendentals=0
        ),
        name="roll_last" if last else "roll_first",
    )(far, *arrays, *extra)


def local(values_in, prob_up, prob_down, discount, swap_rate, annuity, state_price, exercise_step, strike_bucket, notional_sign, strike_table):
    n, total_width = values_in.shape
    steps = prob_up.shape[0]
    node_count = lax.axis_size(NODE)
    trade_count = lax.axis_size("trade")
    rows = n // node_count
    first_width = FIRST_TILES * LANES
    second_width = total_width - first_width
    f32 = jnp.float32
    table = (prob_up, prob_down, discount, swap_rate, annuity)
    price_rows = state_price.reshape(-1, LANES)
    trades = (exercise_step.T, strike_bucket.reshape(-1, LANES), notional_sign.reshape(-1, LANES), strike_table.reshape(1, -1))

    far = (lax.axis_index(NODE) == node_count - 1).astype(jnp.int32).reshape(1)

    arrays = (values_in,) + table + (price_rows,) + trades
    first, first_sums, packed = roll_chunk(0, first_width, jnp.zeros((1,), jnp.int32), arrays, ())
    halo = lax.ppermute(packed, NODE, [((i + 1) % node_count, i) for i in range(node_count)])
    first_moved = lax.all_to_all(first.reshape(node_count, rows, first_width), NODE, 0, 0, tiled=True)
    second, part, sums = roll_chunk(first_width, second_width, far, arrays, (here(halo), first_sums))
    moved_sums = [
        lax.ppermute(sums, "trade", [(i, (i + k) % trade_count) for i in range(trade_count)])
        for k in range(1, trade_count)
    ]
    second = pl.pallas_call(
        tail_kernel,
        in_specs=[HERE] * (trade_count + 1) + [FAR],
        out_specs=FAR,
        out_shape=jax.ShapeDtypeStruct(second.shape, f32),
        scratch_shapes=[vmem(n, LANES), pltpu.SemaphoreType.DMA(())],
        input_output_aliases={trade_count + 1: 0},
        name="tail",
    )(sums, *(here(z) for z in moved_sums), part, second)
    second_moved = lax.all_to_all(
        second.reshape(node_count, rows, second_width + LANES), NODE, 0, 0, tiled=True
    )

    out_shape = jax.ShapeDtypeStruct((rows, node_count * total_width), f32)
    half = pl.pallas_call(
        functools.partial(first_half_kernel, node_count, total_width),
        in_specs=[HERE],
        out_specs=FAR,
        out_shape=out_shape,
        scratch_shapes=[pltpu.SemaphoreType.DMA((node_count,))],
        cost_estimate=pl.CostEstimate(flops=4 * n * total_width, bytes_accessed=8 * n * first_width, transcendentals=0),
        name="first_half",
    )(here(first_moved))
    values, prices, portfolio = pl.pallas_call(
        functools.partial(second_half_kernel, node_count, total_width, steps, float(n)),
        in_specs=[HERE, HERE, FAR],
        out_specs=[FAR, SCALARS, SCALARS],
        out_shape=[out_shape, jax.ShapeDtypeStruct((rows,), f32), jax.ShapeDtypeStruct((1,), f32)],
        scratch_shapes=[
            vmem(rows, node_count * LANES),
            vmem(rows, node_count * second_width),
            pltpu.SemaphoreType.DMA((2, node_count)),
        ],
        input_output_aliases={2: 0},
        name="second_half",
    )(here(first_moved), here(second_moved), half)
    return values, prices, portfolio.reshape(())


def solution(mesh):
    split = Mesh(mesh.devices.reshape(mesh.shape["trade"], 4, 4, 2), TRADE_NODE)
    in_specs = (
        P("trade", NODE),
        P(None, NODE),
        P(None, NODE),
        P(None, NODE),
        P(None, NODE),
        P(None, NODE),
        P(NODE),
        P("trade", None),
        P("trade"),
        P("trade"),
        P(),
    )
    out_specs = (P(TRADE_NODE, None), P(TRADE_NODE), P())

    return jax.shard_map(local, mesh=split, in_specs=in_specs, out_specs=out_specs, check_vma=False)
```

time: 180 us -> 85.2 us (0.47)
  blocking collectives: 68.7 us -> 0 us
  other arithmetic: 35.6 us -> 0 us
  waiting for transfers between devices: 4.27 us -> 35.8 us
  local copies, waits for them, and re-layouts: 31.2 us -> 0.01 us
  Pallas kernels: 0 us -> 27.8 us
  starting transfers between devices: 35.2 us -> 20.5 us
  between operations: 4.02 us -> 0.71 us
    psum x4 -> x0, blocking collectives: 43.3 us -> none  [one_axis_at_a_time(): x = lax.psum(x, axis)]
    pallas_call x0 -> x5, Pallas kernels: none -> 27.8 us  [the longest x2 22.7 us: roll_chunk(): pl.pallas_call(functools.partial(roll_kernel, start, last), in_specs=[SCA...]
    ppermute x10 -> x4, starting transfers between devices: 30.8 us -> 4.83 us  [the longest x3 4.53 us: local(): lax.ppermute(sums, 'trade', [(i, (i + k) % trade_count) for i in range(tr...]
    all_to_all x1 -> x0, blocking collectives: 25.5 us -> none  [summed_on_arrival(): tiles = lax.all_to_all(cut_along(x, dim, devices), axis, 0, 0, tiled=True)]
    select_n x15 -> x0, other arithmetic: 22.2 us -> none  [roll_front(): jnp.where(inside[first_cell:first_cell + cell_count][None, :], rolled, 0.0)]
    ppermute x10 -> x4, waiting for transfers between devices: 4.26 us -> 21.6 us  [the longest x1 18.1 us: local(): lax.ppermute(packed, NODE, [((i + 1) % node_count, i) for i in range(node...]
    all_to_all x1 -> x2, waiting for transfers between devices: 0.01 us -> 14.3 us  [the longest x1 14.3 us: local(): lax.all_to_all(second.reshape(node_count, rows, second_width + LANES), NO...]
    slice x20 -> x0, local copies, waits for them, and re-layouts: 12.6 us -> none  [the longest x9 7.13 us: roll_front(): rolled = roll_once(padded, coefs[0], coefs[1], coefs[2])]
  transfers between devices with their start and end apart: 11 -> 6, of which waited for: 5 -> 4; matrix products, arithmetic and copies ran while one was open for 15% -> 0% of each run, Pallas kernels for 0% -> 15%
where the time goes in v3:
time: 85.2 us; the launch traced here: 84.8 us
  waiting for transfers between devices  35.8 us (42%)
  Pallas kernels  27.8 us (33%)
  starting transfers between devices  20.5 us (24%)
    pallas_call x2, Pallas kernels, roll_chunk(): pl.pallas_call(functools.partial(roll_kernel, start, last), in_specs=[SCA...  22.7 us
    ppermute x1, waiting for transfers between devices, local(): lax.ppermute(packed, NODE, [((i + 1) % node_count, i) for i in range(node...  18.1 us
    all_to_all x1, waiting for transfers between devices, local(): lax.all_to_all(second.reshape(node_count, rows, second_width + LANES), NO...  14.3 us
    all_to_all x1, starting transfers between devices, local(): lax.all_to_all(first.reshape(node_count, rows, first_width), NODE, 0, 0,...  8.72 us
    all_to_all x1, starting transfers between devices, local(): lax.all_to_all(second.reshape(node_count, rows, second_width + LANES), NO...  6.97 us
    ppermute x3, starting transfers between devices, local(): lax.ppermute(sums, 'trade', [(i, (i + k) % trade_count) for i in range(tr...  4.53 us
    ppermute x3, waiting for transfers between devices, local(): lax.ppermute(sums, 'trade', [(i, (i + k) % trade_count) for i in range(tr...  3.47 us
    pallas_call x1, Pallas kernels, local(): pl.pallas_call(functools.partial(second_half_kernel, node_count, total_wi...  2.08 us
  transfers between devices with their start and end apart: 6, of which 4 were waited for; matrix products, arithmetic and copies ran while one was open for 0% of the time, Pallas kernels for 15%

profile of v3, /device:TPU:1, one launch (start us, length us, event | category | flops | bytes accessed | tf_op | source)
XLA Modules:
  0.0 84.8 jit_solution(14908401470321413342)
XLA Ops:
  0.6 12.7 %roll_first.1 = (f32[256,1280]{1,0:T(8,128)}, f32[256,128]{1,0:T(8,128)}, f32[344,128]{1,0:T(8,128)}) custom-call(s32[1]{0:T(128)} %constant.6.clone.1.far_ref, f32[256,2048]{1,0:T(8,128)} %v_ref.3, f32[16,2048]{1,0:T(8,128)} %up_ref.3, f32[16,2048]{1,0:T(8,128)} %dn_ref.3, f32[16,2048]{1,0:T(8,128)} %dc_ref.3, f32[16,2048]{1,0:T(8,128)} %sr_ref.3, ...), custom_call_target="tpu_custom_call" | custom-call | flops 62914560 | bytes 3932160 | tf_op jit(solution)/shard_map/roll_first/pallas_call | solution.py:374
  13.3 0.0 copy-start
  13.3 8.7 %all-to-all-start = ((f32[32,8,1280]{2,1,0:T(8,128)}), f32[32,8,1280]{2,1,0:T(8,128)S(1)}, u32[]{:S(2)}, u32[]{:S(2)}) async-start(f32[32,8,1280]{2,1,0:T(8,128)} %bitcast.10), calls=%async_computation | async-start | bytes 2621440 | tf_op jit(solution)/shard_map/all_to_all | solution.py:430
  22.0 0.0 copy-done
  22.0 0.3 collective-permute-start
  22.3 18.1 %collective-permute-done.rest_5_ = f32[344,128]{1,0:T(8,128)S(1)} collective-permute-done((f32[344,128]{1,0:T(8,128)S(1)}, f32[344,128]{1,0:T(8,128)S(1)}, u32[]{:S(2)}, u32[]{:S(2)}) %collective-permute-start) | collective-permute-done | bytes 176160 | tf_op jit(solution)/shard_map/ppermute | solution.py:429
  40.4 10.1 %roll_last.1 = (f32[256,896]{1,0:T(8,128)}, f32[256,128]{1,0:T(8,128)}, f32[8,128]{1,0:T(8,128)}) custom-call(s32[1]{0:T(128)} %bitcast.6.far_ref, f32[256,2048]{1,0:T(8,128)} %v_ref.3, f32[16,2048]{1,0:T(8,128)} %up_ref.3, f32[16,2048]{1,0:T(8,128)} %dn_ref.3, f32[16,2048]{1,0:T(8,128)} %dc_ref.3, f32[16,2048]{1,0:T(8,128)} %sr_ref.3, f32[16,2048]{1,0:T(8,128)} %an_ref.3, ...), custom_call_target="tpu_custom_call" | custom-call | flops 37748736 | bytes 2359296 | tf_op jit(solution)/shard_map/roll_last/pallas_call | solution.py:374
  50.5 3.8 %collective-permute-start.3 = (f32[8,128]{1,0:T(8,128)}, f32[8,128]{1,0:T(8,128)S(1)}, u32[]{:S(2)}, u32[]{:S(2)}) collective-permute-start(f32[8,128]{1,0:T(8,128)} %get-tuple-element.15.sum_ref), channel_id=1, source_target_pairs={{0,96},{32,0},{64,32},{96,64},{1,97},{33,1},{65,33},{97,65},{2,98}... | collective-permute-start | bytes 12296 | tf_op jit(solution)/shard_map/ppermute | solution.py:433
  54.3 0.0 collective-permute-start.2
  54.3 0.7 collective-permute-start.1
  55.0 0.3 collective-permute-done.3.refs_2_
  55.3 3.2 %collective-permute-done.2.refs_1_ = f32[8,128]{1,0:T(8,128)S(1)} collective-permute-done((f32[8,128]{1,0:T(8,128)}, f32[8,128]{1,0:T(8,128)S(1)}, u32[]{:S(2)}, u32[]{:S(2)}) %collective-permute-start.2) | collective-permute-done | bytes 4128 | tf_op jit(solution)/shard_map/ppermute | solution.py:433
  58.5 0.0 collective-permute-done.1.refs_0_
  58.5 1.7 %tail.1 = f32[256,896]{1,0:T(8,128)} custom-call(f32[8,128]{1,0:T(8,128)} %get-tuple-element.15.sum_ref, f32[8,128]{1,0:T(8,128)S(1)} %collective-permute-done.1.refs_0_, f32[8,128]{1,0:T(8,128)S(1)} %collective-permute-done.2.refs_1_, f32[8,128]{1,0:T(8,128)S(1)} %collective-permute-done.3.refs_2_, ...), custom_call_target="tpu_custom_call", output_to_operand_aliasing={{}: (5, {})} | custom-call | tf_op jit(solution)/shard_map/tail/pallas_call | solution.py:436
  60.2 0.0 all-to-all-done.a_ref
  60.2 7.0 %all-to-all-start.1 = ((f32[32,8,896]{2,1,0:T(8,128)}), f32[32,8,896]{2,1,0:T(8,128)S(1)}, u32[]{:S(2)}, u32[]{:S(2)}) async-start(f32[32,8,896]{2,1,0:T(8,128)} %bitcast.9), calls=%async_computation.1 | async-start | bytes 1835008 | tf_op jit(solution)/shard_map/all_to_all | solution.py:445
  67.2 1.3 %first_half.1.old_ref = f32[8,65536]{1,0:T(8,128)} custom-call(f32[32,8,1280]{2,1,0:T(8,128)S(1)} %all-to-all-done.a_ref), custom_call_target="tpu_custom_call" | custom-call | flops 2097152 | bytes 2621440 | tf_op jit(solution)/shard_map/first_half/pallas_call | solution.py:450
  68.5 14.3 %all-to-all-done.1.b_ref = f32[32,8,896]{2,1,0:T(8,128)S(1)} async-done(((f32[32,8,896]{2,1,0:T(8,128)}), f32[32,8,896]{2,1,0:T(8,128)S(1)}, u32[]{:S(2)}, u32[]{:S(2)}) %all-to-all-start.1) | async-done | bytes 917536 | tf_op jit(solution)/shard_map/all_to_all | solution.py:445
  82.7 2.1 %second_half.1 = (f32[8,65536]{1,0:T(8,128)}, f32[8]{0:T(128)}, f32[1]{0:T(128)}) custom-call(f32[32,8,1280]{2,1,0:T(8,128)S(1)} %all-to-all-done.a_ref, f32[32,8,896]{2,1,0:T(8,128)S(1)} %all-to-all-done.1.b_ref, f32[8,65536]{1,0:T(8,128)} %first_half.1.old_ref), custom_call_target="tpu_custom_call", output_to_operand_aliasing={{0}: (2, {})} | custom-call | tf_op jit(solution)/shard_map/second_half/pallas_call | solution.py:459
Async XLA Ops:
  13.3 8.7 %copy-start = (f32[344,128]{1,0:T(8,128)S(1)}, f32[344,128]{1,0:T(8,128)}, u32[]{:S(2)}) copy-start(f32[344,128]{1,0:T(8,128)} %get-tuple-element.13) | copy-start | bytes 528388
  13.3 46.9 %all-to-all-start = ((f32[32,8,1280]{2,1,0:T(8,128)}), f32[32,8,1280]{2,1,0:T(8,128)S(1)}, u32[]{:S(2)}, u32[]{:S(2)}) async-start(f32[32,8,1280]{2,1,0:T(8,128)} %bitcast.10), calls=%async_computation | async-start | bytes 2621440 | tf_op jit(solution)/shard_map/all_to_all | solution.py:430
  22.0 18.4 %collective-permute-start = (f32[344,128]{1,0:T(8,128)S(1)}, f32[344,128]{1,0:T(8,128)S(1)}, u32[]{:S(2)}, u32[]{:S(2)}) collective-permute-start(f32[344,128]{1,0:T(8,128)S(1)} %copy-done), channel_id=1, source_target_pairs={{1,0},{2,1},{3,2},{4,3},{5,4},{6,5},{7,6},{8,7},{9,8},{10,9},{11,1... | collective-permute-start | bytes 528392 | tf_op jit(solution)/shard_map/ppermute | solution.py:429
  50.5 4.8 %collective-permute-start.3 = (f32[8,128]{1,0:T(8,128)}, f32[8,128]{1,0:T(8,128)S(1)}, u32[]{:S(2)}, u32[]{:S(2)}) collective-permute-start(f32[8,128]{1,0:T(8,128)} %get-tuple-element.15.sum_ref), channel_id=1, source_target_pairs={{0,96},{32,0},{64,32},{96,64},{1,97},{33,1},{65,33},{97,65},{2,98}... | collective-permute-start | bytes 12296 | tf_op jit(solution)/shard_map/ppermute | solution.py:433
  54.3 4.2 %collective-permute-start.2 = (f32[8,128]{1,0:T(8,128)}, f32[8,128]{1,0:T(8,128)S(1)}, u32[]{:S(2)}, u32[]{:S(2)}) collective-permute-start(f32[8,128]{1,0:T(8,128)} %get-tuple-element.15.sum_ref), channel_id=1, source_target_pairs={{0,64},{32,96},{64,0},{96,32},{1,65},{33,97},{65,1},{97,33},{2,66}... | collective-permute-start | bytes 12296 | tf_op jit(solution)/shard_map/ppermute | solution.py:433
  54.3 4.2 %collective-permute-start.1 = (f32[8,128]{1,0:T(8,128)}, f32[8,128]{1,0:T(8,128)S(1)}, u32[]{:S(2)}, u32[]{:S(2)}) collective-permute-start(f32[8,128]{1,0:T(8,128)} %get-tuple-element.15.sum_ref), channel_id=1, source_target_pairs={{0,32},{32,64},{64,96},{96,0},{1,33},{33,65},{65,97},{97,1},{2,34}... | collective-permute-start | bytes 12296 | tf_op jit(solution)/shard_map/ppermute | solution.py:433
  60.2 22.5 %all-to-all-start.1 = ((f32[32,8,896]{2,1,0:T(8,128)}), f32[32,8,896]{2,1,0:T(8,128)S(1)}, u32[]{:S(2)}, u32[]{:S(2)}) async-start(f32[32,8,896]{2,1,0:T(8,128)} %bitcast.9), calls=%async_computation.1 | async-start | bytes 1835008 | tf_op jit(solution)/shard_map/all_to_all | solution.py:445
